TPU v7x, 8 devices: a whole 2x2x1 slice. The times are simulated.
8 devices in a mesh: dp: 2 (over z, y), sp: 4 (over x, core).
Axes of the slice: x: 2, y: 2, z: 1, core: 2. Of those that a mesh axis runs over, the one named last changes fastest.
Arguments:
- tok_in: bfloat16 [4096, 6144], P(('dp', 'sp')), parts along dimension 0
- tok_pos: int32 [4096], P(('dp', 'sp')), parts along dimension 0
- w_dq: bfloat16 [6144, 1536], replicated
- g_q: float32 [1536], replicated
- w_uq: bfloat16 [1536, 64, 192], replicated
- w_dkv: bfloat16 [6144, 576], replicated
- g_kv: float32 [512], replicated
- w_uk: bfloat16 [512, 64, 128], replicated
- w_uv: bfloat16 [512, 64, 128], replicated
- w_o: bfloat16 [64, 128, 6144], replicated
Outputs:
- output 1: bfloat16 [4096, 6144], P(('dp', 'sp')), parts along dimension 0
- output 2: bfloat16 [4096, 512], P(('dp', 'sp')), parts along dimension 0
- output 3: bfloat16 [4096, 64], P(('dp', 'sp')), parts along dimension 0
There are 2 independent parts. A program takes and returns all parts, laid end to end along the dimension named above; an argument that names none is the same for every part.
All inputs are finite; a program needn't handle non-finite values.
Results may differ from a plain program's by a relative error of at most 0.006.
Values are sent between devices in bfloat16 or wider.
A program may use at most 1 GiB of HBM per device.

v0:
```python
import math
import jax
import jax.numpy as jnp
from jax import lax
from jax.sharding import PartitionSpec as P

ROPE_THETA = 10000.0
YARN_FACTOR = 40.0
ORIG_CTX = 4096.0
BETA_FAST = 32.0
BETA_SLOW = 1.0
NORM_EPS = 1e-6


def rope_freqs(rot_dim):
    half_dim = rot_dim // 2
    log_base = 2.0 * math.log(ROPE_THETA)
    low_idx = max(math.floor(rot_dim * math.log(ORIG_CTX / (BETA_FAST * 2.0 * math.pi)) / log_base), 0)
    high_idx = min(math.ceil(rot_dim * math.log(ORIG_CTX / (BETA_SLOW * 2.0 * math.pi)) / log_base), half_dim - 1)
    spread = max(high_idx - low_idx, 0.001)
    freq_list = []
    for freq_idx in range(half_dim):
        base_freq = ROPE_THETA ** (-2.0 * freq_idx / rot_dim)
        ramp_val = min(max((freq_idx - low_idx) / spread, 0.0), 1.0)
        freq_list.append(base_freq / YARN_FACTOR * ramp_val + base_freq * (1.0 - ramp_val))
    return jnp.asarray(freq_list, dtype=jnp.float32)


def rotate_half(act_in, cos_t, sin_t):
    half_dim = act_in.shape[-1] // 2
    first = act_in[..., :half_dim]
    second = act_in[..., half_dim:]
    return jnp.concatenate([first * cos_t - second * sin_t, second * cos_t + first * sin_t], axis=-1)


def rms_norm(act_in, gain):
    mean_sq = jnp.mean(act_in * act_in, axis=-1, keepdims=True)
    return act_in * lax.rsqrt(mean_sq + NORM_EPS) * gain


def solution(mesh):
    groups = mesh.shape['sp']
    tok_spec = P(('dp', 'sp'))
    rows_spec = P(('dp', 'sp'), None)
    replicated = P()

    def local_step(tok_in, tok_pos, w_dq, g_q, w_uq, w_dkv, g_kv, w_uk, w_uv, w_o):
        rows = tok_in.shape[0]
        num_heads = w_uq.shape[1]
        qk_dim = w_uq.shape[2]
        kv_rank = g_kv.shape[0]
        rot_dim = w_dkv.shape[1] - kv_rank
        nope_dim = qk_dim - rot_dim
        v_dim = w_uv.shape[2]
        seq_len = rows * groups
        attn_scale = (0.1 * math.log(YARN_FACTOR) + 1.0) ** 2 / math.sqrt(qk_dim)
        angles = tok_pos.astype(jnp.float32)[:, None] * rope_freqs(rot_dim)[None, :]
        cos_t = jnp.cos(angles)
        sin_t = jnp.sin(angles)
        q_lat = rms_norm(jnp.dot(tok_in, w_dq, preferred_element_type=jnp.float32), g_q).astype(jnp.bfloat16)
        q_full = jnp.einsum('tc,che->the', q_lat, w_uq, preferred_element_type=jnp.float32)
        q_all = jnp.concatenate([q_full[:, :, :nope_dim], rotate_half(q_full[:, :, nope_dim:], cos_t[:, None, :], sin_t[:, None, :])], axis=-1).astype(jnp.bfloat16)
        kv_lat = jnp.dot(tok_in, w_dkv, preferred_element_type=jnp.float32)
        cache_kv = rms_norm(kv_lat[:, :kv_rank], g_kv).astype(jnp.bfloat16)
        cache_pe = rotate_half(kv_lat[:, kv_rank:], cos_t, sin_t).astype(jnp.bfloat16)
        k_nope = jnp.einsum('tc,chn->thn', cache_kv, w_uk, preferred_element_type=jnp.float32).astype(jnp.bfloat16)
        values = jnp.einsum('tc,chv->thv', cache_kv, w_uv, preferred_element_type=jnp.float32).astype(jnp.bfloat16)
        k_all = jnp.concatenate([k_nope, jnp.broadcast_to(cache_pe[:, None, :], (rows, num_heads, rot_dim))], axis=-1)
        q_heads = lax.all_to_all(q_all, 'sp', 1, 0, tiled=True)
        k_heads = lax.all_to_all(k_all, 'sp', 1, 0, tiled=True)
        v_heads = lax.all_to_all(values, 'sp', 1, 0, tiled=True)
        key_idx = jnp.arange(seq_len)

        def block_attention(blk_idx):
            start = blk_idx * rows
            q_blk = lax.dynamic_slice_in_dim(q_heads, start, rows, axis=0)
            logits = jnp.einsum('qhe,khe->hqk', q_blk, k_heads, preferred_element_type=jnp.float32) * attn_scale
            row_idx = start + jnp.arange(rows)
            logits = jnp.where(key_idx[None, None, :] <= row_idx[None, :, None], logits, -jnp.inf)
            attn_prob = jax.nn.softmax(logits, axis=-1).astype(jnp.bfloat16)
            return jnp.einsum('hqk,khv->qhv', attn_prob, v_heads, preferred_element_type=jnp.float32).astype(jnp.bfloat16)

        o_heads = lax.map(block_attention, jnp.arange(groups)).reshape(seq_len, num_heads // groups, v_dim)
        o_local = lax.all_to_all(o_heads, 'sp', 0, 1, tiled=True)
        attn_out = jnp.einsum('thv,hvd->td', o_local, w_o, preferred_element_type=jnp.float32).astype(jnp.bfloat16)
        return attn_out, cache_kv, cache_pe

    return jax.shard_map(local_step, mesh=mesh, in_specs=(rows_spec, tok_spec, replicated, replicated, replicated, replicated, replicated, replicated, replicated, replicated), out_specs=(rows_spec, rows_spec, rows_spec), check_vma=False)
```

profile of v0, /device:TPU:0, one launch (start us, length us, event | category | flops | bytes accessed | tf_op | source)
XLA Modules:
  0.0 853.7 jit_solution(10172127361443325557)
XLA Ops:
  0.6 0.0 copy-start.3
  0.6 0.0 copy-start.6
  0.7 8.1 fusion.37
  8.8 0.1 multiply_reduce_fusion.1
  8.9 0.0 copy-done.3
  8.9 0.1 multiply_convert_fusion.2
  9.0 0.0 copy-done.6
  9.1 0.0 copy-start
  9.1 22.1 %fusion.25 = bf16[512,64,128]{2,0,1:T(8,128)(2,1)} fusion(bf16[512,64,128]{2,1,0:T(8,128)(2,1)S(1)} %copy-done.6, bf16[512,512]{0,1:T(8,128)(2,1)S(1)} %multiply_convert_fusion.2), kind=kOutput, calls=%fused_computation.28 | convolution fusion | flops 4299161600 | bytes 17301504 | tf_op jit(solution)/shard_map/tc,chv->thv/dot_general | solution.py:67
  31.2 0.0 copy-start.4
  31.2 6.2 all-to-all-start.2
  37.4 0.0 copy-done.4
  37.4 0.0 copy-start.7
  37.4 16.9 %multiply_reduce_fusion = (f32[512]{0:T(512)S(1)}, f32[512,1536]{1,0:T(8,128)}) fusion(bf16[512,6144]{1,0:T(8,128)(2,1)} %param.13, bf16[6144,1536]{1,0:T(8,128)(2,1)} %param.15), kind=kOutput, calls=%fused_computation.32 | convolution fusion | flops 9665249280 | bytes 28313600 | tf_op jit(solution)/shard_map/dot_general | solution.py:60
  54.3 0.0 copy-done.7
  54.3 30.0 %fusion.28 = f32[512,12288]{0,1} fusion(bf16[1536,12288]{0,1:T(8,128)(2,1)} %bitcast.62, f32[512,1536]{1,0:T(8,128)} %get-tuple-element.82, f32[1536]{0:T(1024)S(1)} %copy-done.7, f32[512]{0:T(512)S(1)} %add_rsqrt_fusion.1), kind=kOutput, calls=%fused_computation.33 | convolution fusion | flops 19329712128 | bytes 66068480
  84.4 6.7 slice.48
  91.1 0.0 copy-done.5
  91.1 0.3 subtract_convert_fusion.1
  91.4 4.9 subtract_convert_fusion
  96.4 9.3 %pad_maximum_fusion = bf16[512,64,192]{0,2,1:T(8,128)(2,1)} fusion(bf16[512,64,32]{0,2,1:T(8,128)(2,1)S(1)} %get-tuple-element.76, bf16[512,64,32]{0,2,1:T(8,128)(2,1)S(1)} %get-tuple-element.75, bf16[512,64,128]{0,2,1:T(8,128)(2,1)S(1)} %slice.48), kind=kLoop, calls=%fused_computation.23 | loop fusion | flops 37748736 | bytes 25165824 | tf_op jit(solution)/shard_map/concatenate | solution.py:62
  105.7 25.6 %all-to-all-done.2 = bf16[512,64,128]{2,0,1:T(8,128)(2,1)} async-done(((bf16[512,64,128]{2,0,1:T(8,128)(2,1)}), bf16[512,64,128]{2,0,1:T(8,128)(2,1)}, u32[]{:S(2)}, u32[]{:S(2)}) %all-to-all-start.2) | async-done | bytes 8388640 | tf_op jit(solution)/shard_map/all_to_all | solution.py:71
  131.3 6.3 all-to-all-start
  137.6 12.9 %copy.24 = bf16[512,64,128]{0,2,1:T(8,128)(2,1)} copy(bf16[512,64,128]{2,1,0:T(8,128)(2,1)} %param.20) | data formatting | bytes 16777216 | tf_op args[7]
  150.4 0.0 copy-done
  150.4 7.1 fusion.38
  157.5 1.2 convert_element_type.36
  158.8 0.0 copy-start.2
  158.8 0.6 copy-done.2
  159.4 0.5 broadcast_in_dim.16
  159.9 8.3 pad_maximum_fusion.1
  168.2 107.1 %all-to-all-done = bf16[512,64,192]{0,2,1:T(8,128)(2,1)} async-done(((bf16[512,64,192]{0,2,1:T(8,128)(2,1)}), bf16[512,64,192]{0,2,1:T(8,128)(2,1)}, u32[]{:S(2)}, u32[]{:S(2)}) %all-to-all-start) | async-done | bytes 12582944 | tf_op jit(solution)/shard_map/all_to_all | solution.py:69
  275.4 6.5 all-to-all-start.1
  281.9 7.7 copy.28
  289.6 10.8 %copy.37 = bf16[4,16,24,8,512]{4,3,0,2,1:T(8,128)(2,1)} copy(bf16[4,16,24,8,512]{4,3,2,1,0:T(8,128)(2,1)} %bitcast.25) | data formatting | bytes 25165824 | tf_op jit(solution)/shard_map/all_to_all | solution.py:69
  300.4 119.2 %all-to-all-done.1 = bf16[512,64,192]{0,2,1:T(8,128)(2,1)} async-done(((bf16[512,64,192]{0,2,1:T(8,128)(2,1)}), bf16[512,64,192]{0,2,1:T(8,128)(2,1)}, u32[]{:S(2)}, u32[]{:S(2)}) %all-to-all-start.1) | async-done | bytes 12582944 | tf_op jit(solution)/shard_map/all_to_all | solution.py:70
  419.6 10.9 %copy.38 = bf16[4,16,24,8,512]{4,3,0,2,1:T(8,128)(2,1)} copy(bf16[4,16,24,8,512]{4,3,2,1,0:T(8,128)(2,1)} %bitcast.27) | data formatting | bytes 25165824 | tf_op jit(solution)/shard_map/all_to_all | solution.py:70
  430.5 254.1 %while.11 = (s32[]{:T(128)}, bf16[4,512,16,128]{3,2,1,0:T(8,128)(2,1)}, s32[4]{0:T(128)S(1)}, bf16[2048,16,192]{0,2,1:T(8,128)(2,1)}, bf16[2048,16,192]{0,2,1:T(...) while((s32[]{:T(128)}, ...), condition=%wide.region_5.6_spmd.clone, body=%wide.region_2.5_spmd.clone.sunk | while | flops 10840180736 | bytes 166793888 | solution.py:83
  430.5 0.6 dynamic_slice.24
  431.8 0.7 iota_compare_fusion.2
  432.4 33.6 %fusion.58 = (f32[16,512]{1,0:T(8,128)S(1)}, f32[16,512,2048]{2,1,0:T(8,128)}) fusion(pred[512,2048]{1,0:T(8,128)(4,1)S(1)} %iota_compare_fusion.2, bf16[2048,16,192]{0,2,1:T(8,128)(2,1)} %get-tuple-element.148, bf16[2048,16,192]{0,2,1:T(8,128)(2,1)} %get-tuple-element.147, s32[]{:T(128)S(6)} %select_n.22), kind=kOutput, calls=%fused_computation.46.clone.1 | convolution fusion | flops 6509561856 | bytes 83918848 | tf_op jit(solution)/shard_map/while/body/eval_jaxpr/sub | solution.py:80
  466.1 25.3 %convert_bitcast_fusion.2 = bf16[1,512,16,128]{3,1,2,0:T(8,128)(2,1)S(1)} fusion(bf16[2048,16,128]{2,0,1:T(8,128)(2,1)} %get-tuple-element.149, f32[16,512,2048]{2,1,0:T(8,128)} %get-tuple-element.122, f32[16,512]{1,0:T(8,128)S(1)} %get-tuple-element.123), kind=kOutput, calls=%fused_computation.16.clone.1 | convolution fusion | flops 4329570304 | bytes 77627392 | tf_op jit(solution)/shard_map/while/body/eval_jaxpr/hqk,khv->qhv/dot_general | solution.py:81
  491.3 2.7 copy_dynamic-update-slice_fusion.2
  494.0 0.6 dynamic_slice.24
  495.3 0.7 iota_compare_fusion.2
  495.9 33.6 %fusion.58 = (f32[16,512]{1,0:T(8,128)S(1)}, f32[16,512,2048]{2,1,0:T(8,128)}) fusion(pred[512,2048]{1,0:T(8,128)(4,1)S(1)} %iota_compare_fusion.2, bf16[2048,16,192]{0,2,1:T(8,128)(2,1)} %get-tuple-element.148, bf16[2048,16,192]{0,2,1:T(8,128)(2,1)} %get-tuple-element.147, s32[]{:T(128)S(6)} %select_n.22), kind=kOutput, calls=%fused_computation.46.clone.1 | convolution fusion | flops 6509561856 | bytes 83918848 | tf_op jit(solution)/shard_map/while/body/eval_jaxpr/sub | solution.py:80
  529.5 25.3 %convert_bitcast_fusion.2 = bf16[1,512,16,128]{3,1,2,0:T(8,128)(2,1)S(1)} fusion(bf16[2048,16,128]{2,0,1:T(8,128)(2,1)} %get-tuple-element.149, f32[16,512,2048]{2,1,0:T(8,128)} %get-tuple-element.122, f32[16,512]{1,0:T(8,128)S(1)} %get-tuple-element.123), kind=kOutput, calls=%fused_computation.16.clone.1 | convolution fusion | flops 4329570304 | bytes 77627392 | tf_op jit(solution)/shard_map/while/body/eval_jaxpr/hqk,khv->qhv/dot_general | solution.py:81
  554.8 2.7 copy_dynamic-update-slice_fusion.2
  557.5 0.6 dynamic_slice.24
  558.8 0.7 iota_compare_fusion.2
  559.4 33.6 %fusion.58 = (f32[16,512]{1,0:T(8,128)S(1)}, f32[16,512,2048]{2,1,0:T(8,128)}) fusion(pred[512,2048]{1,0:T(8,128)(4,1)S(1)} %iota_compare_fusion.2, bf16[2048,16,192]{0,2,1:T(8,128)(2,1)} %get-tuple-element.148, bf16[2048,16,192]{0,2,1:T(8,128)(2,1)} %get-tuple-element.147, s32[]{:T(128)S(6)} %select_n.22), kind=kOutput, calls=%fused_computation.46.clone.1 | convolution fusion | flops 6509561856 | bytes 83918848 | tf_op jit(solution)/shard_map/while/body/eval_jaxpr/sub | solution.py:80
  593.1 25.2 %convert_bitcast_fusion.2 = bf16[1,512,16,128]{3,1,2,0:T(8,128)(2,1)S(1)} fusion(bf16[2048,16,128]{2,0,1:T(8,128)(2,1)} %get-tuple-element.149, f32[16,512,2048]{2,1,0:T(8,128)} %get-tuple-element.122, f32[16,512]{1,0:T(8,128)S(1)} %get-tuple-element.123), kind=kOutput, calls=%fused_computation.16.clone.1 | convolution fusion | flops 4329570304 | bytes 77627392 | tf_op jit(solution)/shard_map/while/body/eval_jaxpr/hqk,khv->qhv/dot_general | solution.py:81
  618.3 2.7 copy_dynamic-update-slice_fusion.2
  621.0 0.6 dynamic_slice.24
  622.3 0.7 iota_compare_fusion.2
  623.0 33.6 %fusion.58 = (f32[16,512]{1,0:T(8,128)S(1)}, f32[16,512,2048]{2,1,0:T(8,128)}) fusion(pred[512,2048]{1,0:T(8,128)(4,1)S(1)} %iota_compare_fusion.2, bf16[2048,16,192]{0,2,1:T(8,128)(2,1)} %get-tuple-element.148, bf16[2048,16,192]{0,2,1:T(8,128)(2,1)} %get-tuple-element.147, s32[]{:T(128)S(6)} %select_n.22), kind=kOutput, calls=%fused_computation.46.clone.1 | convolution fusion | flops 6509561856 | bytes 83918848 | tf_op jit(solution)/shard_map/while/body/eval_jaxpr/sub | solution.py:80
  656.6 25.3 %convert_bitcast_fusion.2 = bf16[1,512,16,128]{3,1,2,0:T(8,128)(2,1)S(1)} fusion(bf16[2048,16,128]{2,0,1:T(8,128)(2,1)} %get-tuple-element.149, f32[16,512,2048]{2,1,0:T(8,128)} %get-tuple-element.122, f32[16,512]{1,0:T(8,128)S(1)} %get-tuple-element.123), kind=kOutput, calls=%fused_computation.16.clone.1 | convolution fusion | flops 4329570304 | bytes 77627392 | tf_op jit(solution)/shard_map/while/body/eval_jaxpr/hqk,khv->qhv/dot_general | solution.py:81
  681.8 2.7 copy_dynamic-update-slice_fusion.2
  684.6 6.0 all-to-all-start.3
  690.6 0.0 copy-done.1
  690.6 1.0 copy.31
  691.6 91.8 %all-to-all-done.3 = bf16[2048,16,128]{2,1,0:T(8,128)(2,1)} async-done(((bf16[2048,16,128]{2,1,0:T(8,128)(2,1)}), bf16[2048,16,128]{2,1,0:T(8,128)(2,1)}, u32[]{:S(2)}, u32[]{:S(2)}) %all-to-all-start.3) | async-done | bytes 8388640 | tf_op jit(solution)/shard_map/all_to_all | solution.py:84
  783.4 8.8 %copy.30 = bf16[512,4,16,128]{3,0,2,1:T(8,128)(2,1)} copy(bf16[512,4,16,128]{3,2,0,1:T(8,128)(2,1)} %bitcast.14) | data formatting | bytes 16777216 | tf_op jit(solution)/shard_map/all_to_all | solution.py:84
  792.2 61.1 %bitcast_convert_fusion = bf16[512,6144]{1,0:T(8,128)(2,1)} fusion(bf16[512,64,128]{2,0,1:T(8,128)(2,1)} %bitcast.61, bf16[64,128,6144]{2,1,0:T(8,128)(2,1)} %param.22), kind=kOutput, calls=%fused_computation.25 | convolution fusion | flops 51542753280 | bytes 115343360 | tf_op jit(solution)/shard_map/thv,hvd->td/dot_general | solution.py:85
  (12 shorter events, 0.0 us)
Async XLA Ops:
  0.6 8.3 copy-start.3
  0.6 8.4 copy-start.6
  9.1 141.4 %copy-start = (bf16[512,512]{0,1:T(8,128)(2,1)}, bf16[512,512]{0,1:T(8,128)(2,1)S(1)}, u32[]{:S(2)}) copy-start(bf16[512,512]{0,1:T(8,128)(2,1)S(1)} %multiply_convert_fusion.2) | copy-start | bytes 1572868
  31.2 6.2 copy-start.4
  31.2 100.1 %all-to-all-start.2 = ((bf16[512,64,128]{2,0,1:T(8,128)(2,1)}), bf16[512,64,128]{2,0,1:T(8,128)(2,1)}, u32[]{:S(2)}, u32[]{:S(2)}) async-start(bf16[512,64,128]{2,0,1:T(8,128)(2,1)} %fusion.25), calls=%async_computation.2 | async-start | bytes 16777216 | tf_op jit(solution)/shard_map/all_to_all | solution.py:71
  37.4 16.9 %copy-start.7 = (f32[1536]{0:T(1024)S(1)}, f32[1536]{0:T(1024)}, u32[]{:S(2)}) copy-start(f32[1536]{0:T(1024)} %param.16) | copy-start | bytes 18436
  84.4 6.7 copy-start.5
  131.3 144.1 %all-to-all-start = ((bf16[512,64,192]{0,2,1:T(8,128)(2,1)}), bf16[512,64,192]{0,2,1:T(8,128)(2,1)}, u32[]{:S(2)}, u32[]{:S(2)}) async-start(bf16[512,64,192]{0,2,1:T(8,128)(2,1)} %pad_maximum_fusion), calls=%async_computation | async-start | bytes 25165824 | tf_op jit(solution)/shard_map/all_to_all | solution.py:69
  158.8 0.6 copy-start.2
  275.4 144.3 %all-to-all-start.1 = ((bf16[512,64,192]{0,2,1:T(8,128)(2,1)}), bf16[512,64,192]{0,2,1:T(8,128)(2,1)}, u32[]{:S(2)}, u32[]{:S(2)}) async-start(bf16[512,64,192]{0,2,1:T(8,128)(2,1)} %pad_maximum_fusion.1), calls=%async_computation.1 | async-start | bytes 25165824 | tf_op jit(solution)/shard_map/all_to_all | solution.py:70
  684.6 6.0 copy-start.1
  684.6 98.8 %all-to-all-start.3 = ((bf16[2048,16,128]{2,1,0:T(8,128)(2,1)}), bf16[2048,16,128]{2,1,0:T(8,128)(2,1)}, u32[]{:S(2)}, u32[]{:S(2)}) async-start(bf16[2048,16,128]{2,1,0:T(8,128)(2,1)} %bitcast.60), calls=%async_computation.3 | async-start | bytes 16777216 | tf_op jit(solution)/shard_map/all_to_all | solution.py:84
where the time goes:
time: 863 us; the launch traced here: 854 us
  matrix products  381 us (44%)
  waiting for transfers between devices  344 us (40%)
  local copies, waits for them, and re-layouts  73.2 us (8%)
  other arithmetic  27.1 us (3%)
  starting transfers between devices  25 us (3%)
    sub x4, matrix products, block_attention(): attn_prob = jax.nn.softmax(logits, axis=-1).astype(jnp.bfloat16)  134 us
    all_to_all x1, waiting for transfers between devices, local_step(): k_heads = lax.all_to_all(k_all, 'sp', 1, 0, tiled=True)  119 us
    all_to_all x1, waiting for transfers between devices, local_step(): q_heads = lax.all_to_all(q_all, 'sp', 1, 0, tiled=True)  107 us
    dot_general x4, matrix products, block_attention(): jnp.einsum('hqk,khv->qhv', attn_prob, v_heads, preferred_element_type=jnp...  101 us
    all_to_all x1, waiting for transfers between devices, local_step(): o_local = lax.all_to_all(o_heads, 'sp', 0, 1, tiled=True)  91.8 us
    dot_general x1, matrix products, local_step(): jnp.einsum('thv,hvd->td', o_local, w_o, preferred_element_type=jnp.float32)  61.1 us
    unnamed x2, matrix products  37.1 us
    all_to_all x1, waiting for transfers between devices, local_step(): v_heads = lax.all_to_all(values, 'sp', 1, 0, tiled=True)  25.6 us
  transfers between devices with their start and end apart: 4, of which 4 were waited for; matrix products, arithmetic and copies ran while one was open for 14% of the time, Pallas kernels for 0%

commit v1 on v0

v1 whole, which is shorter than its diff:
```python
import math
import jax
import jax.numpy as jnp
from jax import lax
from jax.experimental import pallas as pl
from jax.experimental.pallas import tpu as pltpu
from jax.sharding import PartitionSpec as P

ROPE_THETA = 10000.0
YARN_FACTOR = 40.0
ORIG_CTX = 4096.0
BETA_FAST = 32.0
BETA_SLOW = 1.0
NORM_EPS = 1e-6
BF = jnp.bfloat16
F32 = jnp.float32


def rope_freqs(rot_dim):
    half_dim = rot_dim // 2
    log_base = 2.0 * math.log(ROPE_THETA)
    low_idx = max(math.floor(rot_dim * math.log(ORIG_CTX / (BETA_FAST * 2.0 * math.pi)) / log_base), 0)
    high_idx = min(math.ceil(rot_dim * math.log(ORIG_CTX / (BETA_SLOW * 2.0 * math.pi)) / log_base), half_dim - 1)
    spread = max(high_idx - low_idx, 0.001)
    freq_list = []
    for freq_idx in range(half_dim):
        base_freq = ROPE_THETA ** (-2.0 * freq_idx / rot_dim)
        ramp_val = min(max((freq_idx - low_idx) / spread, 0.0), 1.0)
        freq_list.append(base_freq / YARN_FACTOR * ramp_val + base_freq * (1.0 - ramp_val))
    return jnp.asarray(freq_list, dtype=F32)


def attn_kernel(scale, info, wq, wk, wv, cq_m, cq_o, cs_m, cs_o, ckv, ckvt, pe, o_m, o_o, kbuf, vbuf, qbuf, sbuf, m_ref, l_ref, acc):
    me = info[0]
    n_pieces = info[1]
    rows = cq_m.shape[1]

    @pl.when(pl.program_id(0) == 0)
    def _():
        qbuf[:, :, 192:, :] = jnp.zeros_like(qbuf[:, :, 192:, :])

        @pl.loop(0, n_pieces)
        def _(c):
            slot = jnp.bitwise_and(me - c, 3)
            for h in range(2):
                kbuf[h, c, :, 128:] = pe[slot]

    for idx, (cq, cs) in enumerate(((cq_m, cs_m), (cq_o, cs_o))):
        cos, sin = cs[:32], cs[32:]
        u = jnp.dot(wq[...], cq[...], preferred_element_type=F32)
        for h in range(2):
            b = 192 * h
            z1, z2 = u[b + 128:b + 160], u[b + 160:b + 192]
            qbuf[idx, h, 0:128] = u[b:b + 128].astype(BF)
            qbuf[idx, h, 128:160] = (z1 * cos - z2 * sin).astype(BF)
            qbuf[idx, h, 160:192] = (z2 * cos + z1 * sin).astype(BF)

    wk2 = jnp.concatenate([wk[0], wk[1]], axis=1)
    wv2 = wv[...].reshape(256, wv.shape[2])

    @pl.loop(0, n_pieces)
    def _(c):
        slot = jnp.bitwise_and(me - c, 3)
        kn = jnp.dot(ckv[slot], wk2, preferred_element_type=F32).astype(BF)
        kbuf[0, c, :, :128] = kn[:, :128]
        kbuf[1, c, :, :128] = kn[:, 128:]
        vbuf[c] = jnp.dot(wv2, ckvt[slot], preferred_element_type=F32).astype(BF)

    def scores(idx, h, c):
        return jnp.dot(kbuf[h, c], qbuf[idx, h], preferred_element_type=F32)

    def absorb(h, c, s):
        m_old = m_ref[h]
        m_new = jnp.maximum(m_old, jnp.max(s, axis=0, keepdims=True))
        alpha = jnp.exp2((m_old - m_new) * scale)
        p = jnp.exp2((s - m_new) * scale)
        m_ref[h] = m_new
        l_ref[h] = l_ref[h] * alpha + jnp.sum(p.reshape(rows // 8, 8, rows), axis=0)
        acc[h] = acc[h] * alpha + jnp.dot(vbuf[c, 128 * h:128 * h + 128], p.astype(BF), preferred_element_type=F32)

    for idx, out in enumerate((o_m, o_o)):
        piece = info[2 + idx]
        m_ref[...] = jnp.full_like(m_ref, -jnp.inf)
        l_ref[...] = jnp.zeros_like(l_ref)
        acc[...] = jnp.zeros_like(acc)
        for h in range(2):
            sbuf[0, h] = scores(idx, h, 0)

        @pl.loop(0, piece)
        def _(j):
            now = jnp.bitwise_and(j, 1)
            for h in range(2):
                sbuf[1 - now, h] = scores(idx, h, j + 1)
            for h in range(2):
                absorb(h, j, sbuf[now, h])

        last = jnp.bitwise_and(piece, 1)
        keep = lax.broadcasted_iota(jnp.int32, (rows, rows), 0) <= lax.broadcasted_iota(jnp.int32, (rows, rows), 1)
        for h in range(2):
            absorb(h, piece, jnp.where(keep, sbuf[last, h], -jnp.inf))
            total = jnp.sum(l_ref[h], axis=0, keepdims=True)
            o_t = (acc[h] * (1.0 / total)).astype(BF)
            out[:, 128 * h:128 * h + 128] = o_t.T


def out_kernel(info, a, b, wa, wb, y):
    r = jnp.dot(a[...], wa[...], preferred_element_type=F32) + jnp.dot(b[...], wb[...], preferred_element_type=F32)
    y[...] = r.astype(BF)


def solution(mesh):
    groups = mesh.shape['sp']
    tok_spec = P(('dp', 'sp'))
    rows_spec = P(('dp', 'sp'), None)
    rep = P()

    def shift(x, k):
        return lax.ppermute(x, 'sp', [(i, (i + k) % groups) for i in range(groups)])

    def swap(x):
        return lax.ppermute(x, 'sp', [(i, i ^ 1) for i in range(groups)])

    def local_step(tok_in, tok_pos, w_dq, g_q, w_uq, w_dkv, g_kv, w_uk, w_uv, w_o):
        rows, width = tok_in.shape
        heads, qk_dim = w_uq.shape[1], w_uq.shape[2]
        q_rank, kv_rank = w_dq.shape[1], g_kv.shape[0]
        v_dim = w_uv.shape[2]
        rot = w_dkv.shape[1] - kv_rank
        half = rot // 2
        own = heads // 2
        pairs = own // 2
        scale = (0.1 * math.log(YARN_FACTOR) + 1.0) ** 2 / math.sqrt(qk_dim) * math.log2(math.e)
        me = lax.axis_index('sp')
        core = me % 2

        angles = tok_pos.astype(F32)[None, :] * rope_freqs(rot)[:, None]
        cs = jnp.concatenate([jnp.cos(angles), jnp.sin(angles)], axis=0)
        cos_t, sin_t = cs[:half].T, cs[half:].T
        kv = jnp.dot(tok_in, w_dkv, preferred_element_type=F32)
        a, b1, b2 = kv[:, :kv_rank], kv[:, kv_rank:kv_rank + half], kv[:, kv_rank + half:]
        cache_kv = (a * lax.rsqrt(jnp.mean(a * a, axis=-1, keepdims=True) + NORM_EPS) * g_kv).astype(BF)
        cache_pe = jnp.concatenate([b1 * cos_t - b2 * sin_t, b2 * cos_t + b1 * sin_t], axis=-1).astype(BF)
        lat = jnp.concatenate([cache_kv, cache_pe, jnp.zeros((rows, 128 - rot), BF)], axis=1)
        lats = jnp.stack([lat] + [shift(lat, k) for k in range(1, groups)])
        cs_o = swap(cs)

        uq = jnp.dot(tok_in, w_dq, preferred_element_type=F32)
        c_q = (uq * lax.rsqrt(jnp.mean(uq * uq, axis=-1, keepdims=True) + NORM_EPS) * g_q).astype(BF).T
        cq_o = swap(c_q)

        ckv = lats[:, :, :kv_rank]
        pe = lats[:, :, kv_rank:]
        ckvt = jnp.swapaxes(ckv, 1, 2)
        wq_t = jnp.transpose(w_uq, (1, 2, 0)).reshape(heads * qk_dim, q_rank)
        wk_h = jnp.transpose(lax.dynamic_slice_in_dim(w_uk, core * own, own, axis=1), (1, 0, 2))
        wv_h = jnp.transpose(lax.dynamic_slice_in_dim(w_uv, core * own, own, axis=1), (1, 2, 0))
        info = jnp.stack([me, 2 * (me // 2) + 2, me, me ^ 1, core]).astype(jnp.int32)
        full = pl.BlockSpec(memory_space=pltpu.VMEM)
        o_m, o_o = pl.pallas_call(
            lambda *r: attn_kernel(scale, *r),
            grid_spec=pltpu.PrefetchScalarGridSpec(
                num_scalar_prefetch=1,
                grid=(pairs,),
                in_specs=[
                    pl.BlockSpec((2 * qk_dim, q_rank), lambda p, i: (i[4] * pairs + p, 0)),
                    pl.BlockSpec((2, kv_rank, 128), lambda p, i: (p, 0, 0)),
                    pl.BlockSpec((2, 128, kv_rank), lambda p, i: (p, 0, 0)),
                ] + [full] * 7,
                out_specs=[pl.BlockSpec((rows, 2 * v_dim), lambda p, i: (0, p))] * 2,
                scratch_shapes=[
                    pltpu.VMEM((2, groups, rows, 256), BF),
                    pltpu.VMEM((groups, 2 * v_dim, rows), BF),
                    pltpu.VMEM((2, 2, 256, rows), BF),
                    pltpu.VMEM((2, 2, rows, rows), F32),
                    pltpu.VMEM((2, 1, rows), F32),
                    pltpu.VMEM((2, 8, rows), F32),
                    pltpu.VMEM((2, v_dim, rows), F32),
                ],
            ),
            out_shape=[jax.ShapeDtypeStruct((rows, own * v_dim), BF)] * 2,
            compiler_params=pltpu.CompilerParams(dimension_semantics=("arbitrary",), vmem_limit_bytes=56 << 20),
            cost_estimate=pl.CostEstimate(flops=90 * 10 ** 9, bytes_accessed=60 << 20, transcendentals=10 ** 8),
            name="attn",
        )(info, wq_t, wk_h, wv_h, c_q, cq_o, cs, cs_o, ckv, ckvt, pe)
        o_r = swap(o_o)
        bn = 512
        depth = own * v_dim
        attn_out = pl.pallas_call(
            out_kernel,
            grid_spec=pltpu.PrefetchScalarGridSpec(
                num_scalar_prefetch=1,
                grid=(width // bn,),
                in_specs=[full, full,
                          pl.BlockSpec((depth, bn), lambda n, i: (i[4], n)),
                          pl.BlockSpec((depth, bn), lambda n, i: (1 - i[4], n))],
                out_specs=pl.BlockSpec((rows, bn), lambda n, i: (0, n)),
            ),
            out_shape=jax.ShapeDtypeStruct((rows, width), BF),
            compiler_params=pltpu.CompilerParams(dimension_semantics=("arbitrary",), vmem_limit_bytes=56 << 20),
            cost_estimate=pl.CostEstimate(flops=52 * 10 ** 9, bytes_accessed=110 << 20, transcendentals=0),
            name="outproj",
        )(info, o_m, o_r, w_o.reshape(heads * v_dim, width), w_o.reshape(heads * v_dim, width))
        return attn_out, cache_kv, cache_pe

    return jax.shard_map(local_step, mesh=mesh, in_specs=(rows_spec, tok_spec) + (rep,) * 8, out_specs=(rows_spec,) * 3, check_vma=False)
```

time: 863 us -> 319 us (0.37)
  the two profiles are of different devices: /device:TPU:0 before, /device:TPU:7 now
where the time goes in v1:
time: 319 us
  Pallas kernels  248 us (78%)
  local copies, waits for them, and re-layouts  28.5 us (9%)
  matrix products  23.1 us (7%)
  other arithmetic  9.23 us (3%)
  waiting for transfers between devices  5.96 us (2%)
  starting transfers between devices  3.56 us (1%)
    pallas_call x1, Pallas kernels, local_step(): pl.pallas_call(lambda *r: attn_kernel(scale, *r), grid_spec=pltpu.Prefetc...  186 us
    pallas_call x1, Pallas kernels, local_step(): pl.pallas_call(out_kernel, grid_spec=pltpu.PrefetchScalarGridSpec(num_sca...  61.5 us
    unnamed x27, local copies, waits for them, and re-layouts  13.4 us
    dot_general x1, matrix products, local_step(): uq = jnp.dot(tok_in, w_dq, preferred_element_type=F32)  13.4 us
    dot_general x1, matrix products, local_step(): kv = jnp.dot(tok_in, w_dkv, preferred_element_type=F32)  9.74 us
  transfers between devices with their start and end apart: 6, of which 1 were waited for; matrix products, arithmetic and copies ran while one was open for 14% of the time, Pallas kernels for 0%

profile of v1, /device:TPU:7, one launch (start us, length us, event | category | flops | bytes accessed | tf_op | source)
XLA Modules:
  0.0 318.9 jit_solution(15372997733800987020)
XLA Ops:
  0.6 0.0 slice-start
  0.6 0.8 convert_element_type.16
  1.5 0.0 copy-start.5
  1.5 0.0 copy-start.4
  1.5 0.0 slice-start.1
  1.5 0.0 slice-start.2
  1.5 0.0 slice-start.3
  1.5 0.0 slice-start.4
  1.5 9.7 %fusion.9 = f32[512,576]{1,0:T(8,128)S(1)} fusion(bf16[512,6144]{1,0:T(8,128)(2,1)} %param.11, bf16[6144,576]{0,1:T(8,128)(2,1)} %param.16), kind=kOutput, calls=%fused_computation.28 | convolution fusion | flops 3623878656 | bytes 14548992 | tf_op jit(solution)/shard_map/dot_general | solution.py:139
  11.3 0.1 multiply_reduce_fusion.1
  11.4 0.1 pad.9.clone
  11.5 0.0 copy-done.5
  11.5 1.2 fusion.6
  12.7 0.0 copy-done.4
  12.7 0.2 multiply_convert_fusion.1
  12.9 0.0 copy-start
  12.9 0.8 copy-done
  13.7 1.0 maximum_maximum_fusion
  14.7 0.3 collective-permute-start.3
  15.0 2.0 collective-permute-start.2
  17.0 0.0 collective-permute-start.4
  17.0 0.0 slice-done
  17.0 0.0 slice-done.1
  17.0 0.0 slice-done.2
  17.0 0.0 slice-done.3
  17.0 0.0 slice-done.4
  17.1 13.4 %multiply_reduce_fusion = (f32[512]{0:T(512)S(1)}, f32[512,1536]{1,0:T(8,128)}) fusion(bf16[512,6144]{1,0:T(8,128)(2,1)} %param.11, bf16[6144,1536]{1,0:T(8,128)(2,1)S(1)} %bitcast.29), kind=kOutput, calls=%fused_computation.2 | convolution fusion | flops 9665249280 | bytes 28313600 | tf_op jit(solution)/shard_map/dot_general | solution.py:147
  30.5 0.0 copy-start.3
  30.5 2.4 copy.24
  32.9 0.0 copy-done.3
  32.9 1.5 fusion.r_4_
  34.4 0.6 collective-permute-start
  35.0 0.3 multiply_cosine_fusion.1
  35.4 0.0 copy-start.2
  35.4 0.0 collective-permute-start.1
  35.4 2.9 constant_dynamic-slice_fusion.1
  38.4 0.0 copy-done.2
  38.4 3.6 %copy.35 = bf16[512,32,128]{2,0,1:T(8,128)(2,1)} copy(bf16[512,32,128]{2,1,0:T(8,128)(2,1)S(1)} %constant_dynamic-slice_fusion.1) | data formatting | bytes 8388608
  42.0 4.9 %constant_dynamic-slice_fusion = bf16[512,32,128]{2,1,0:T(8,128)(2,1)} fusion(bf16[512,64,128]{2,1,0:T(8,128)(2,1)} %param.19, s32[]{:T(128)S(6)} %select_n.17), kind=kLoop, calls=%fused_computation.25 | loop fusion | bytes 8388612 | tf_op jit(solution)/shard_map/dynamic_slice | solution.py:156
  47.0 0.0 copy-start.1
  47.0 7.6 %copy.33 = bf16[512,32,128]{0,2,1:T(8,128)(2,1)} copy(bf16[512,32,128]{2,1,0:T(8,128)(2,1)} %constant_dynamic-slice_fusion) | data formatting | bytes 8388608
  54.6 0.6 stack.35.r_0_.info
  55.2 0.0 copy-done.1
  55.2 0.2 fusion.14
  55.4 0.0 collective-permute-done.3
  55.4 0.0 collective-permute-done.2
  55.4 0.0 collective-permute-done.4
  55.4 1.9 pad_maximum_fusion
  57.3 1.7 slice_bitcast_fusion
  59.0 2.4 copy.29.r_9_
  61.4 1.9 pad_maximum_fusion.1.r_10_
  63.3 0.0 collective-permute-done.1.r_7_
  63.3 0.0 copy-start.6
  63.3 0.0 collective-permute-done.r_5_
  63.3 0.6 copy-done.6
  63.9 186.0 %attn.1 = (bf16[512,4096]{1,0:T(8,128)(2,1)}, bf16[512,4096]{1,0:T(8,128)(2,1)}) custom-call(s32[5]{0:T(128)} %stack.35.r_0_.info, bf16[12288,1536]{1,0:T(8,128)(2,1)} %bitcast.27, bf16[32,512,128]{2,1,0:T(8,128)(2,1)} %bitcast.25, bf16[32,128,512]{2,1,0:T(8,128)(2,1)} %bitcast.26, bf16[1536,512]{1,0:T(8,128)(2,1)} %fusion.r_4_, ...), custom_call_target="tpu_custom_call" | custom-call | flops 89999998976 | bytes 62914560 | tf_op jit(solution)/shard_map/attn/pallas_call | solution.py:159
  249.9 0.6 collective-permute-start.5
  250.5 0.1 pad_maximum_fusion.3
  250.6 0.7 copy.30
  251.4 5.9 %collective-permute-done.5.b = bf16[512,4096]{1,0:T(8,128)(2,1)} collective-permute-done((bf16[512,4096]{1,0:T(8,128)(2,1)}, bf16[512,4096]{1,0:T(8,128)(2,1)}, u32[]{:S(2)}, u32[]{:S(2)}) %collective-permute-start.5) | collective-permute-done | bytes 4194336 | tf_op jit(solution)/shard_map/ppermute | solution.py:121
  257.3 61.5 %outproj.1 = bf16[512,6144]{1,0:T(8,128)(2,1)} custom-call(s32[5]{0:T(128)} %stack.35.r_0_.info, bf16[512,4096]{1,0:T(8,128)(2,1)} %get-tuple-element.5.a, bf16[512,4096]{1,0:T(8,128)(2,1)} %collective-permute-done.5.b, bf16[8192,6144]{1,0:T(8,128)(2,1)} %bitcast.14.wa.wb, bf16[8192,6144]{1,0:T(8,128)(2,1)} %bitcast.14.wa.wb), custom_call_target="tpu_custom_call" | custom-call | flops 51999997952 | bytes 115343360 | tf_op jit(solution)/shard_map/outproj/pallas_call | solution.py:188
  (5 shorter events, 0.0 us)
Async XLA Ops:
  0.6 16.4 %slice-start = ((s8[18874368]{0:T(1024)(128)(4,1)}), s8[4194304]{0:T(1024)(128)(4,1)S(1)}, s32[]{:S(2)}) async-start(s8[18874368]{0:T(1024)(128)(4,1)} %bitcast.28), calls=%async_computation | async-start | bytes 8388608
  1.5 10.0 %copy-start.5 = (f32[32]{0:T(128)S(1)}, f32[32]{0:T(128)}, u32[]{:S(2)}) copy-start(f32[32]{0:T(128)} %constant.48.clone) | copy-start | bytes 388
  1.5 11.2 %copy-start.4 = (f32[512]{0:T(512)S(1)}, f32[512]{0:T(512)}, u32[]{:S(2)}) copy-start(f32[512]{0:T(512)} %param.17) | copy-start | bytes 6148
  1.5 15.5 %slice-start.1 = ((s8[18874368]{0:T(1024)(128)(4,1)}), s8[4194304]{0:T(1024)(128)(4,1)S(1)}, s32[]{:S(2)}) async-start(s8[18874368]{0:T(1024)(128)(4,1)} %bitcast.28), calls=%async_computation.1 | async-start | bytes 8388608
  1.5 15.5 %slice-start.2 = ((s8[18874368]{0:T(1024)(128)(4,1)}), s8[4194304]{0:T(1024)(128)(4,1)S(1)}, s32[]{:S(2)}) async-start(s8[18874368]{0:T(1024)(128)(4,1)} %bitcast.28), calls=%async_computation.2 | async-start | bytes 8388608
  1.5 15.5 %slice-start.3 = ((s8[18874368]{0:T(1024)(128)(4,1)}), s8[4194304]{0:T(1024)(128)(4,1)S(1)}, s32[]{:S(2)}) async-start(s8[18874368]{0:T(1024)(128)(4,1)} %bitcast.28), calls=%async_computation.3 | async-start | bytes 8388608
  1.5 15.5 %slice-start.4 = ((s8[18874368]{0:T(1024)(128)(4,1)}), s8[2097152]{0:T(1024)(128)(4,1)S(1)}, s32[]{:S(2)}) async-start(s8[18874368]{0:T(1024)(128)(4,1)} %bitcast.28), calls=%async_computation.4 | async-start | bytes 4194304
  12.9 0.8 copy-start
  14.7 40.7 %collective-permute-start.3 = (bf16[512,640]{1,0:T(8,128)(2,1)}, bf16[512,640]{1,0:T(8,128)(2,1)}, u32[]{:S(2)}, u32[]{:S(2)}) collective-permute-start(bf16[512,640]{1,0:T(8,128)(2,1)} %maximum_maximum_fusion), channel_id=1, source_target_pairs={{0,2},{1,3},{2,0},{3,1},{4,6},{5,7},{6,4},{7,5}} | collective-permute-start | bytes 1966088 | tf_op jit(solution)/shard_map/ppermute | solution.py:118
  15.0 40.4 %collective-permute-start.2 = (bf16[512,640]{1,0:T(8,128)(2,1)}, bf16[512,640]{1,0:T(8,128)(2,1)}, u32[]{:S(2)}, u32[]{:S(2)}) collective-permute-start(bf16[512,640]{1,0:T(8,128)(2,1)} %maximum_maximum_fusion), channel_id=1, source_target_pairs={{0,1},{1,2},{2,3},{3,0},{4,5},{5,6},{6,7},{7,4}} | collective-permute-start | bytes 1966088 | tf_op jit(solution)/shard_map/ppermute | solution.py:118
  17.0 38.4 %collective-permute-start.4 = (bf16[512,640]{1,0:T(8,128)(2,1)}, bf16[512,640]{1,0:T(8,128)(2,1)}, u32[]{:S(2)}, u32[]{:S(2)}) collective-permute-start(bf16[512,640]{1,0:T(8,128)(2,1)} %maximum_maximum_fusion), channel_id=1, source_target_pairs={{0,3},{1,0},{2,1},{3,2},{4,7},{5,4},{6,5},{7,6}} | collective-permute-start | bytes 1966088 | tf_op jit(solution)/shard_map/ppermute | solution.py:118
  30.5 2.4 copy-start.3
  34.4 28.9 %collective-permute-start = (bf16[1536,512]{1,0:T(8,128)(2,1)}, bf16[1536,512]{1,0:T(8,128)(2,1)}, u32[]{:S(2)}, u32[]{:S(2)}) collective-permute-start(bf16[1536,512]{1,0:T(8,128)(2,1)} %fusion.r_4_), channel_id=1, source_target_pairs={{0,1},{1,0},{2,3},{3,2},{4,5},{5,4},{6,7},{7,6}} | collective-permute-start | bytes 4718600 | tf_op jit(solution)/shard_map/ppermute | solution.py:121
  35.4 3.0 copy-start.2
  35.4 27.9 %collective-permute-start.1 = (f32[64,512]{1,0:T(8,128)S(1)}, f32[64,512]{1,0:T(8,128)S(1)}, u32[]{:S(2)}, u32[]{:S(2)}) collective-permute-start(f32[64,512]{1,0:T(8,128)S(1)} %pad_maximum_fusion.2.r_6_), channel_id=1, source_target_pairs={{0,1},{1,0},{2,3},{3,2},{4,5},{5,4},{6,7},{7,6}} | collective-permute-start | bytes 393224 | tf_op jit(solution)/shard_map/ppermute | solution.py:121
  47.0 8.2 %copy-start.1 = (bf16[512,512]{1,0:T(8,128)(2,1)S(1)}, bf16[512,512]{1,0:T(8,128)(2,1)}, u32[]{:S(2)}) copy-start(bf16[512,512]{1,0:T(8,128)(2,1)} %copy-done) | copy-start | bytes 1572868
  63.3 0.6 copy-start.6
  249.9 7.4 %collective-permute-start.5 = (bf16[512,4096]{1,0:T(8,128)(2,1)}, bf16[512,4096]{1,0:T(8,128)(2,1)}, u32[]{:S(2)}, u32[]{:S(2)}) collective-permute-start(bf16[512,4096]{1,0:T(8,128)(2,1)} %get-tuple-element.6), channel_id=1, source_target_pairs={{0,1},{1,0},{2,3},{3,2},{4,5},{5,4},{6,7},{7,6}} | collective-permute-start | bytes 12582920 | tf_op jit(solution)/shard_map/ppermute | solution.py:121

commit v2 on v0

v2 whole, which is shorter than its diff:
```python
import math
import jax
import jax.numpy as jnp
from jax import lax
from jax.experimental import pallas as pl
from jax.experimental.pallas import tpu as pltpu
from jax.sharding import PartitionSpec as P

ROPE_THETA = 10000.0
YARN_FACTOR = 40.0
ORIG_CTX = 4096.0
BETA_FAST = 32.0
BETA_SLOW = 1.0
NORM_EPS = 1e-6
BF = jnp.bfloat16
F32 = jnp.float32


def rope_freqs(rot_dim):
    half_dim = rot_dim // 2
    log_base = 2.0 * math.log(ROPE_THETA)
    low_idx = max(math.floor(rot_dim * math.log(ORIG_CTX / (BETA_FAST * 2.0 * math.pi)) / log_base), 0)
    high_idx = min(math.ceil(rot_dim * math.log(ORIG_CTX / (BETA_SLOW * 2.0 * math.pi)) / log_base), half_dim - 1)
    spread = max(high_idx - low_idx, 0.001)
    freq_list = []
    for freq_idx in range(half_dim):
        base_freq = ROPE_THETA ** (-2.0 * freq_idx / rot_dim)
        ramp_val = min(max((freq_idx - low_idx) / spread, 0.0), 1.0)
        freq_list.append(base_freq / YARN_FACTOR * ramp_val + base_freq * (1.0 - ramp_val))
    return jnp.asarray(freq_list, dtype=F32)


def attn_kernel(scale, n_q, n_dep, info, *refs):
    wq, wk, wv = refs[:3]
    lats = refs[3:7]
    cqs = refs[7:7 + n_q]
    cs = refs[7 + n_q]
    o_m, o_o, ckv, cqv, kbuf, vbuf, qbuf, sbuf, m_ref, l_ref, acc, sems = refs[8 + n_q + n_dep:]
    me, n_pieces, p_m, p_o, skip, q_slot = (info[k] for k in range(6))
    rows = cqv.shape[2]
    step = pl.program_id(0)

    @pl.when(step == 0)
    def _():
        def fetch(base):
            return [pltpu.make_async_copy(cqs[base + k], cqv.at[k], sems.at[k]) for k in range(2)]

        for base in range(0, n_q, 2):
            @pl.when(q_slot == base)
            def _():
                for c in fetch(base):
                    c.start()
        copies = [pltpu.make_async_copy(lats[k], ckv.at[jnp.bitwise_xor(me, k)], sems.at[2 + k]) for k in range(4)]
        for c in copies:
            c.start()
        for c in copies + fetch(0):
            c.wait()
        qbuf[:, :, 192:, :] = jnp.zeros_like(qbuf[:, :, 192:, :])

        @pl.loop(0, n_pieces)
        def _(c):
            for h in range(2):
                kbuf[h, c, :, 128:] = ckv[c, :, 512:]

    def item(i):
        st = (i > p_m).astype(jnp.int32)
        return st, i - st * (p_m + 1)

    def qk(slot, st, c):
        for h in range(2):
            sbuf[slot, h] = jnp.dot(kbuf[h, c], qbuf[st, h], preferred_element_type=F32)

    def absorb(slot, st, c, masked):
        for h in range(2):
            s = sbuf[slot, h]
            if masked:
                keep = lax.broadcasted_iota(jnp.int32, (rows, rows), 0) <= lax.broadcasted_iota(jnp.int32, (rows, rows), 1)
                s = jnp.where(keep, s, -jnp.inf)
            m_old = m_ref[st, h]
            m_new = jnp.maximum(m_old, jnp.max(s, axis=0, keepdims=True))
            alpha = jnp.exp2((m_old - m_new) * scale)
            p = jnp.exp2((s - m_new) * scale)
            m_ref[st, h] = m_new
            l_ref[st, h] = l_ref[st, h] * alpha + jnp.sum(p.reshape(rows // 8, 8, rows), axis=0)
            acc[st, h] = acc[st, h] * alpha + jnp.dot(vbuf[c, 128 * h:128 * h + 128], p.astype(BF), preferred_element_type=F32)

    @pl.when(step >= skip)
    def _():
        @pl.loop(0, 2)
        def _(k):
            t = cs[q_slot + k]
            cos, sin = t[:32], t[32:]
            u = jnp.dot(wq[...], cqv[k], preferred_element_type=F32)
            for h in range(2):
                b = 192 * h
                z1, z2 = u[b + 128:b + 160], u[b + 160:b + 192]
                qbuf[k, h, 0:128] = u[b:b + 128].astype(BF)
                qbuf[k, h, 128:160] = (z1 * cos - z2 * sin).astype(BF)
                qbuf[k, h, 160:192] = (z2 * cos + z1 * sin).astype(BF)

        wkv = jnp.concatenate([wk[0], wk[1], wv[0], wv[1]], axis=1)

        @pl.loop(0, n_pieces)
        def _(c):
            kv = jnp.dot(ckv[c, :, :512], wkv, preferred_element_type=F32).astype(BF)
            kbuf[0, c, :, :128] = kv[:, :128]
            kbuf[1, c, :, :128] = kv[:, 128:256]
            vbuf[c] = kv[:, 256:].T

        m_ref[...] = jnp.full_like(m_ref, -jnp.inf)
        l_ref[...] = jnp.zeros_like(l_ref)
        acc[...] = jnp.zeros_like(acc)
        last = p_m + p_o + 1
        qk(0, 0, 0)

        @pl.loop(0, last)
        def _(i):
            now = jnp.bitwise_and(i, 1)
            st, c = item(i)
            st1, c1 = item(i + 1)
            diag = c == jnp.where(st == 0, p_m, p_o)

            def body(masked):
                qk(1 - now, st1, c1)
                absorb(now, st, c, masked)

            @pl.when(diag)
            def _():
                body(True)

            @pl.when(jnp.logical_not(diag))
            def _():
                body(False)

        absorb(jnp.bitwise_and(last, 1), 1, p_o, True)
        for st, out in ((0, o_m), (1, o_o)):
            for h in range(2):
                total = jnp.sum(l_ref[st, h], axis=0, keepdims=True)
                out[:, 128 * h:128 * h + 128] = (acc[st, h] * (1.0 / total)).astype(BF).T


def out_kernel(info, a_a, a_c, b_m, r_m, s_a, s_c, s_b, r_o, wa, wb, y, buf, sems):
    late = info[0] >= 2
    rows, seg = buf.shape[0] // 2, buf.shape[1] // 4

    def cols(ref, k):
        return ref.at[:, pl.ds(k * seg, seg)]

    @pl.when(pl.program_id(0) == 0)
    def _():
        def plan(is_late):
            mine = [cols(a_a, 1), b_m if is_late else cols(a_c, 0), cols(a_c, 1), r_m if is_late else cols(a_a, 0)]
            other = [cols(s_a, 1), s_b if is_late else cols(s_c, 0), cols(s_c, 1), r_o if is_late else cols(s_a, 0)]
            return [pltpu.make_async_copy(src, buf.at[pl.ds(g * rows, rows), pl.ds(k * seg, seg)], sems.at[4 * g + k])
                    for g, part in enumerate((mine, other)) for k, src in enumerate(part)]

        for is_late in (False, True):
            @pl.when(late == is_late)
            def _():
                for c in plan(is_late):
                    c.start()
        for c in plan(False):
            c.wait()

    half = rows // 2

    @pl.loop(0, 2)
    def _(k):
        r = jnp.dot(buf[pl.ds(k * half, half)], wa[...], preferred_element_type=F32) + jnp.dot(buf[pl.ds(rows + k * half, half)], wb[...], preferred_element_type=F32)
        y[pl.ds(k * half, half)] = r.astype(BF)


def solution(mesh):
    groups = mesh.shape['sp']
    tok_spec = P(('dp', 'sp'))
    rows_spec = P(('dp', 'sp'), None)
    rep = P()

    def xor(x, k, sources=range(4)):
        return lax.ppermute(x, 'sp', [(i, i ^ k) for i in sources])

    def run(tok_in, tok_pos, w_dq, g_q, w_uq, w_dkv, g_kv, w_uk, w_uv, w_o):
        rows, width = tok_in.shape
        heads, qk_dim = w_uq.shape[1], w_uq.shape[2]
        q_rank, kv_rank = w_dq.shape[1], g_kv.shape[0]
        v_dim = w_uv.shape[2]
        rot = w_dkv.shape[1] - kv_rank
        half = rot // 2
        own = heads // 2
        pairs = own // 2
        moved = 4
        scale = (0.1 * math.log(YARN_FACTOR) + 1.0) ** 2 / math.sqrt(qk_dim) * math.log2(math.e)
        me = lax.axis_index('sp')
        core = jnp.bitwise_and(me, 1)
        late = me >= 2

        pos = jnp.stack([tok_pos] + [xor(tok_pos, k) for k in range(1, 4)])
        angles = pos.astype(F32)[:, None, :] * rope_freqs(rot)[None, :, None]
        cs = jnp.concatenate([jnp.cos(angles), jnp.sin(angles)], axis=1)
        my_angles = tok_pos.astype(F32)[:, None] * rope_freqs(rot)[None, :]
        cos_t, sin_t = jnp.cos(my_angles), jnp.sin(my_angles)
        kv = jnp.dot(tok_in, w_dkv, preferred_element_type=F32)
        a, b1, b2 = kv[:, :kv_rank], kv[:, kv_rank:kv_rank + half], kv[:, kv_rank + half:]
        cache_kv = (a * lax.rsqrt(jnp.mean(a * a, axis=-1, keepdims=True) + NORM_EPS) * g_kv).astype(BF)
        cache_pe = jnp.concatenate([b1 * cos_t - b2 * sin_t, b2 * cos_t + b1 * sin_t], axis=-1).astype(BF)
        lat = jnp.concatenate([cache_kv, cache_pe, jnp.zeros((rows, 128 - rot), BF)], axis=1)
        lat_x = xor(lat, 2)
        lats = [lat, xor(lat, 1), lat_x, xor(lat_x, 1)]

        tok_in, lat = lax.optimization_barrier((tok_in, lat))
        uq = jnp.dot(tok_in, w_dq, preferred_element_type=F32)
        inv = lax.rsqrt(jnp.mean(uq * uq, axis=-1, keepdims=True) + NORM_EPS)
        c_q = (uq * inv * g_q).astype(BF).T
        cq_o = xor(c_q, 1)
        cq_x = xor(c_q, 2, (2, 3))
        cq_y = xor(c_q, 3, (2, 3))

        wq_t = jnp.transpose(w_uq, (1, 2, 0)).reshape(heads * qk_dim, q_rank)
        wk_h = jnp.transpose(lax.dynamic_slice_in_dim(w_uk, core * own, own, axis=1), (1, 0, 2))
        wv_h = jnp.transpose(lax.dynamic_slice_in_dim(w_uv, core * own, own, axis=1), (1, 0, 2))
        full = pl.BlockSpec(memory_space=pltpu.VMEM)
        hbm = pl.BlockSpec(memory_space=pl.ANY)

        def attend(steps, early_pair, late_pair, late_skip, foreign, *deps):
            pair0 = jnp.where(late, late_pair, early_pair)
            skip = jnp.where(late, late_skip, 0)
            if foreign:
                base = jnp.where(late, me, me ^ 2)
                pieces = jnp.full((), 4, jnp.int32)
                slot = jnp.where(late, 0, 2)
                cqs = [c_q, cq_o, cq_x, cq_y]
            else:
                base, pieces, slot = me, jnp.where(late, 4, 2), jnp.zeros((), jnp.int32)
                cqs = [c_q, cq_o]
            info = jnp.stack([me, pieces, base, base ^ 1, skip, slot, pair0, core]).astype(jnp.int32)

            def pair(p, i):
                return jnp.bitwise_and(i[6] + jnp.maximum(p, i[4]), pairs - 1)

            return pl.pallas_call(
                lambda *r: attn_kernel(scale, len(cqs), len(deps), *r),
                grid_spec=pltpu.PrefetchScalarGridSpec(
                    num_scalar_prefetch=1,
                    grid=(steps,),
                    in_specs=[
                        pl.BlockSpec((2 * qk_dim, q_rank), lambda p, i: (i[7] * pairs + pair(p, i), 0)),
                        pl.BlockSpec((2, kv_rank, v_dim), lambda p, i: (pair(p, i), 0, 0)),
                        pl.BlockSpec((2, kv_rank, v_dim), lambda p, i: (pair(p, i), 0, 0)),
                    ] + [hbm] * (4 + len(cqs)) + [full] + [hbm] * len(deps),
                    out_specs=[pl.BlockSpec((rows, 2 * v_dim), lambda p, i: (0, p))] * 2,
                    scratch_shapes=[
                        pltpu.VMEM((groups, rows, kv_rank + 128), BF),
                        pltpu.VMEM((2, q_rank, rows), BF),
                        pltpu.VMEM((2, groups, rows, 256), BF),
                        pltpu.VMEM((groups, 2 * v_dim, rows), BF),
                        pltpu.VMEM((2, 2, 256, rows), BF),
                        pltpu.VMEM((2, 2, rows, rows), F32),
                        pltpu.VMEM((2, 2, 1, rows), F32),
                        pltpu.VMEM((2, 2, 8, rows), F32),
                        pltpu.VMEM((2, 2, v_dim, rows), F32),
                        pltpu.SemaphoreType.DMA((6,)),
                    ],
                ),
                out_shape=[jax.ShapeDtypeStruct((rows, steps * 2 * v_dim), BF)] * 2,
                compiler_params=pltpu.CompilerParams(dimension_semantics=("arbitrary",), vmem_limit_bytes=48 << 20),
                cost_estimate=pl.CostEstimate(flops=5 * steps * 10 ** 9, bytes_accessed=2 * steps << 20, transcendentals=10 ** 7),
            )(info, wq_t, wk_h, wv_h, *lats, *cqs, cs, *deps)

        a_m, a_o = attend(8, pairs - moved, pairs - moved, moved, False)
        s_a = xor(a_o, 1)
        b_m, b_o = attend(moved, pairs - moved, 4, 0, True, a_m)
        r_m = xor(b_m, 2, (0, 1))
        r_o = xor(b_o, 3, (0, 1))
        s_b = xor(b_o, 1, (2, 3))
        c_m, c_o = attend(8, 4, 4, moved, False, b_m)
        s_c = xor(c_o, 1)
        bn = 512
        depth = own * v_dim
        info = jnp.stack([me, core]).astype(jnp.int32)
        w_o2 = w_o.reshape(heads * v_dim, width)
        attn_out = pl.pallas_call(
            out_kernel,
            grid_spec=pltpu.PrefetchScalarGridSpec(
                num_scalar_prefetch=1,
                grid=(width // bn,),
                in_specs=[hbm] * 8 + [
                    pl.BlockSpec((depth, bn), lambda n, i: (i[1], n)),
                    pl.BlockSpec((depth, bn), lambda n, i: (1 - i[1], n))],
                out_specs=pl.BlockSpec((rows, bn), lambda n, i: (0, n)),
                scratch_shapes=[pltpu.VMEM((2 * rows, depth), BF), pltpu.SemaphoreType.DMA((8,))],
            ),
            out_shape=jax.ShapeDtypeStruct((rows, width), BF),
            compiler_params=pltpu.CompilerParams(dimension_semantics=("arbitrary",), vmem_limit_bytes=56 << 20),
            cost_estimate=pl.CostEstimate(flops=52 * 10 ** 9, bytes_accessed=110 << 20, transcendentals=0),
            name="outproj",
        )(info, a_m, c_m, b_m, r_m, s_a, s_c, s_b, r_o, w_o2, w_o2)
        return attn_out, cache_kv, cache_pe

    return jax.shard_map(run, mesh=mesh, in_specs=(rows_spec, tok_spec) + (rep,) * 8, out_specs=(rows_spec,) * 3, check_vma=False)
```

time: 863 us -> 369 us (0.43)
  matrix products: 381 us -> 23.1 us
  waiting for transfers between devices: 344 us -> 64.7 us
  Pallas kernels: 0 us -> 230 us
  local copies, waits for them, and re-layouts: 73.2 us -> 26.2 us
  other arithmetic: 27.1 us -> 7.85 us
  starting transfers between devices: 25 us -> 15 us
    all_to_all x4 -> x0, waiting for transfers between devices: 344 us -> none  [the longest x1 119 us: local_step(): k_heads = lax.all_to_all(k_all, 'sp', 1, 0, tiled=True)]
    pallas_call x0 -> x4, Pallas kernels: none -> 230 us  [the longest x3 164 us: attend(): pl.pallas_call(lambda *r: attn_kernel(scale, len(cqs), len(deps), *r), gr...]
    dot_general x8 -> x2, matrix products: 209 us -> 23.1 us  [the longest x1 13.4 us: run(): uq = jnp.dot(tok_in, w_dq, preferred_element_type=F32)]
    sub x4 -> x0, matrix products: 134 us -> none  [block_attention(): attn_prob = jax.nn.softmax(logits, axis=-1).astype(jnp.bfloat16)]
    ppermute x0 -> x14, waiting for transfers between devices: none -> 64.7 us  [xor(): return lax.ppermute(x, 'sp', [(i, i ^ k) for i in sources])]
    all_to_all x4 -> x0, local copies, waits for them, and re-layouts: 38.2 us -> none  [the longest x1 10.9 us: local_step(): k_heads = lax.all_to_all(k_all, 'sp', 1, 0, tiled=True)]
    unnamed x2 -> x0, matrix products: 37.1 us -> none
    all_to_all x4 -> x0, starting transfers between devices: 25 us -> none  [the longest x1 6.51 us: local_step(): k_heads = lax.all_to_all(k_all, 'sp', 1, 0, tiled=True)]
  transfers between devices with their start and end apart: 4 -> 14, of which waited for: 4 -> 4; matrix products, arithmetic and copies ran while one was open for 14% -> 6% of each run, Pallas kernels for 0% -> 15%
where the time goes in v2:
time: 369 us; the launch traced here: 368 us
  Pallas kernels  230 us (62%)
  waiting for transfers between devices  64.7 us (18%)
  local copies, waits for them, and re-layouts  26.2 us (7%)
  matrix products  23.1 us (6%)
  starting transfers between devices  15 us (4%)
  other arithmetic  7.85 us (2%)
    pallas_call x3, Pallas kernels, attend(): pl.pallas_call(lambda *r: attn_kernel(scale, len(cqs), len(deps), *r), gr...  164 us
    pallas_call x1, Pallas kernels, run(): pl.pallas_call(out_kernel, grid_spec=pltpu.PrefetchScalarGridSpec(num_sca...  66.5 us
    ppermute x14, waiting for transfers between devices, xor(): return lax.ppermute(x, 'sp', [(i, i ^ k) for i in sources])  64.7 us
    ppermute x14, starting transfers between devices, xor(): return lax.ppermute(x, 'sp', [(i, i ^ k) for i in sources])  15 us
    unnamed x51, local copies, waits for them, and re-layouts  13.7 us
    dot_general x1, matrix products, run(): uq = jnp.dot(tok_in, w_dq, preferred_element_type=F32)  13.4 us
    dot_general x1, matrix products, run(): kv = jnp.dot(tok_in, w_dkv, preferred_element_type=F32)  9.73 us
    dynamic_slice x1, local copies, waits for them, and re-layouts, run(): lax.dynamic_slice_in_dim(w_uv, core * own, own, axis=1)  8.58 us
  transfers between devices with their start and end apart: 14, of which 4 were waited for; matrix products, arithmetic and copies ran while one was open for 6% of the time, Pallas kernels for 15%

profile of v2, /device:TPU:0, one launch (start us, length us, event | category | flops | bytes accessed | tf_op | source)
XLA Modules:
  0.0 368.1 jit_solution(9109171101020594771)
XLA Ops:
  0.6 0.0 slice-start
  0.6 0.8 convert_element_type.22
  1.5 0.0 slice-start.3
  1.5 0.0 slice-start.4
  1.5 9.7 %fusion.9 = f32[512,576]{1,0:T(8,128)S(1)} fusion(bf16[512,6144]{1,0:T(8,128)(2,1)} %param.12, bf16[6144,576]{0,1:T(8,128)(2,1)} %param.17), kind=kOutput, calls=%fused_computation.28 | convolution fusion | flops 3623878656 | bytes 14548992 | tf_op jit(solution)/shard_map/dot_general | solution.py:202
  11.2 0.1 multiply_reduce_fusion.1
  11.4 0.1 pad.11.clone
  11.5 0.0 copy-done.16
  11.5 1.2 fusion.6
  12.7 0.0 copy-done.15
  12.7 0.0 copy-start.9
  12.7 0.2 multiply_convert_fusion.1
  12.9 0.0 copy-start.8
  12.9 0.2 maximum_maximum_fusion.r_4_
  13.2 13.4 %multiply_reduce_fusion = (f32[512]{0:T(512)S(1)}, f32[512,1536]{1,0:T(8,128)}) fusion(bf16[512,6144]{1,0:T(8,128)(2,1)} %param.12, bf16[6144,1536]{1,0:T(8,128)(2,1)S(1)} %bitcast.40), kind=kOutput, calls=%fused_computation.3 | convolution fusion | flops 9665249280 | bytes 28313600 | tf_op jit(solution)/shard_map/dot_general | solution.py:211
  26.6 0.0 copy-start.13
  26.6 3.5 copy.28
  30.1 2.2 fusion.r_8_
  32.4 0.9 collective-permute-start.3
  33.3 2.5 collective-permute-start.1
  35.7 0.2 collective-permute-start.4
  35.9 0.0 collective-permute-start.6
  35.9 1.9 collective-permute-start.5
  37.9 0.0 collective-permute-done.4
  37.9 0.0 collective-permute-start
  37.9 13.3 %collective-permute-done.1.r_6_ = bf16[512,640]{1,0:T(8,128)(2,1)S(1)} collective-permute-done((bf16[512,640]{1,0:T(8,128)(2,1)S(1)}, bf16[512,640]{1,0:T(8,128)(2,1)S(1)}, u32[]{:S(2)}, u32[]{:S(2)}) %collective-permute-start.1) | collective-permute-done | bytes 655392 | tf_op jit(solution)/shard_map/ppermute | solution.py:180
  51.2 0.0 collective-permute-start.2
  51.2 8.6 %constant_dynamic-slice_fusion = (bf16[512,32,128]{2,1,0:T(8,128)(2,1)}, bf16[512,32,128]{2,1,0:T(8,128)(2,1)}) fusion(bf16[512,64,128]{2,1,0:T(8,128)(2,1)} %param.20, s32[]{:T(128)S(6)} %select_n.28, bf16[512,64,128]{2,1,0:T(8,128)(2,1)} %param.19), kind=kLoop, calls=%fused_computation.26 | loop fusion | bytes 16777220 | tf_op jit(solution)/shard_map/dynamic_slice | solution.py:220
  59.7 0.1 stack.80.r_0_
  59.8 0.1 stack.74.r_0_
  59.9 5.9 %copy.35 = bf16[512,32,128]{2,0,1:T(8,128)(2,1)} copy(bf16[512,32,128]{2,1,0:T(8,128)(2,1)} %get-tuple-element.29) | data formatting | bytes 8388608
  65.8 3.6 copy.36
  69.5 0.1 stack.85.r_0_
  69.6 0.0 collective-permute-done.6
  69.6 1.3 collective-permute-start.8
  70.9 0.0 collective-permute-done.5
  70.9 1.3 collective-permute-start.7
  72.2 0.7 add_convert_fusion
  72.9 1.6 multiply_cosine_fusion
  74.6 0.0 collective-permute-done.r_5_
  74.6 0.0 collective-permute-done.2.r_7_
  74.6 0.0 collective-permute-done.3.r_9_
  74.6 55.3 %shard_map.139 = (bf16[512,2048]{1,0:T(8,128)(2,1)}, bf16[512,2048]{1,0:T(8,128)(2,1)}) custom-call(s32[8]{0:T(128)S(1)} %stack.74.r_0_, bf16[12288,1536]{1,0:T(8,128)(2,1)} %bitcast.36, bf16[32,512,128]{2,1,0:T(8,128)(2,1)} %bitcast.32, bf16[32,512,128]{2,1,0:T(8,128)(2,1)} %bitcast.29, bf16[512,640]{1,0:T(8,128)(2,1)S(1)} %maximum_maximum_fusion.r_4_, ...), custom_call_target="tpu_custom_call" | custom-call | flops 40000000000 | bytes 16777216 | tf_op jit(solution)/shard_map/pallas_call | solution.py:240
  129.9 0.0 collective-permute-done.8.r_11_
  130.0 11.9 %collective-permute-done.7.r_10_ = bf16[1536,512]{1,0:T(8,128)(2,1)S(1)} collective-permute-done((bf16[1536,512]{1,0:T(8,128)(2,1)S(1)}, bf16[1536,512]{1,0:T(8,128)(2,1)S(1)}, u32[]{:S(2)}, u32[]{:S(2)}) %collective-permute-start.7) | collective-permute-done | bytes 1572896 | tf_op jit(solution)/shard_map/ppermute | solution.py:180
  141.9 1.2 copy-done.18
  143.0 1.1 copy-done.4
  144.1 1.1 copy-done.6
  145.2 53.3 %shard_map.140 = (bf16[512,1024]{1,0:T(8,128)(2,1)S(1)}, bf16[512,1024]{1,0:T(8,128)(2,1)S(1)}) custom-call(s32[8]{0:T(128)S(1)} %stack.85.r_0_, bf16[12288,1536]{1,0:T(8,128)(2,1)} %bitcast.37, bf16[32,512,128]{2,1,0:T(8,128)(2,1)} %bitcast.33, bf16[32,512,128]{2,1,0:T(8,128)(2,1)} %bitcast.30, bf16[512,640]{1,0:T(8,128)(2,1)S(1)} %maximum_maximum_fusion.r_4_, ...), custom_call_target="tpu_custom_call" | custom-call | flops 20000000000 | bytes 8388608 | tf_op jit(solution)/shard_map/pallas_call | solution.py:240
  198.6 55.0 %shard_map.141 = (bf16[512,2048]{1,0:T(8,128)(2,1)}, bf16[512,2048]{1,0:T(8,128)(2,1)}) custom-call(s32[8]{0:T(128)S(1)} %stack.80.r_0_, bf16[12288,1536]{1,0:T(8,128)(2,1)} %bitcast.38, bf16[32,512,128]{2,1,0:T(8,128)(2,1)} %bitcast.34, bf16[32,512,128]{2,1,0:T(8,128)(2,1)} %bitcast.31, bf16[512,640]{1,0:T(8,128)(2,1)S(1)} %maximum_maximum_fusion.r_4_, ...), custom_call_target="tpu_custom_call" | custom-call | flops 40000000000 | bytes 16777216 | tf_op jit(solution)/shard_map/pallas_call | solution.py:240
  253.6 0.0 collective-permute-start.11
  253.6 0.5 collective-permute-start.10
  254.1 2.5 collective-permute-start.13
  256.6 1.6 collective-permute-start.12
  258.3 2.3 collective-permute-start.9
  260.5 0.1 pad_maximum_fusion.1
  260.7 0.7 copy.29
  261.4 0.6 pad_add_fusion.info
  262.0 17.2 %collective-permute-done.13.r_o = bf16[512,1024]{1,0:T(8,128)(2,1)} collective-permute-done((bf16[512,1024]{1,0:T(8,128)(2,1)S(1)}, bf16[512,1024]{1,0:T(8,128)(2,1)}, u32[]{:S(2)}, u32[]{:S(2)}) %collective-permute-start.13) | collective-permute-done | bytes 1048608 | tf_op jit(solution)/shard_map/ppermute | solution.py:180
  279.2 0.0 collective-permute-done.12.s_b
  279.2 22.3 %collective-permute-done.9.r_m = bf16[512,1024]{1,0:T(8,128)(2,1)} collective-permute-done((bf16[512,1024]{1,0:T(8,128)(2,1)S(1)}, bf16[512,1024]{1,0:T(8,128)(2,1)}, u32[]{:S(2)}, u32[]{:S(2)}) %collective-permute-start.9) | collective-permute-done | bytes 1048608 | tf_op jit(solution)/shard_map/ppermute | solution.py:180
  301.5 0.0 collective-permute-done.11.s_c
  301.5 0.0 collective-permute-done.10.s_a
  301.5 66.5 %outproj.1 = bf16[512,6144]{1,0:T(8,128)(2,1)} custom-call(s32[2]{0:T(128)} %pad_add_fusion.info, bf16[512,2048]{1,0:T(8,128)(2,1)} %get-tuple-element.11.r_13_.a_a, bf16[512,2048]{1,0:T(8,128)(2,1)} %get-tuple-element.13.a_c, bf16[512,1024]{1,0:T(8,128)(2,1)} %copy-done.2, bf16[512,1024]{1,0:T(8,128)(2,1)} %collective-permute-done.9.r_m, ...), custom_call_target="tpu_custom_call" | custom-call | flops 51999997952 | bytes 115343360 | tf_op jit(solution)/shard_map/outproj/pallas_call | solution.py:281
  (42 shorter events, 0.1 us)
Async XLA Ops:
  0.6 12.5 %slice-start = ((s8[18874368]{0:T(1024)(128)(4,1)}), s8[4194304]{0:T(1024)(128)(4,1)S(1)}, s32[]{:S(2)}) async-start(s8[18874368]{0:T(1024)(128)(4,1)} %bitcast.39), calls=%async_computation | async-start | bytes 8388608
  1.5 10.0 %copy-start.16 = (f32[32]{0:T(128)S(1)}, f32[32]{0:T(128)}, u32[]{:S(2)}) copy-start(f32[32]{0:T(128)} %constant.40.clone) | copy-start | bytes 388
  1.5 11.2 %copy-start.15 = (f32[512]{0:T(512)S(1)}, f32[512]{0:T(512)}, u32[]{:S(2)}) copy-start(f32[512]{0:T(512)} %param.18) | copy-start | bytes 6148
  1.5 11.6 %slice-start.1 = ((s8[18874368]{0:T(1024)(128)(4,1)}), s8[4194304]{0:T(1024)(128)(4,1)S(1)}, s32[]{:S(2)}) async-start(s8[18874368]{0:T(1024)(128)(4,1)} %bitcast.39), calls=%async_computation.1 | async-start | bytes 8388608
  1.5 11.6 %slice-start.2 = ((s8[18874368]{0:T(1024)(128)(4,1)}), s8[4194304]{0:T(1024)(128)(4,1)S(1)}, s32[]{:S(2)}) async-start(s8[18874368]{0:T(1024)(128)(4,1)} %bitcast.39), calls=%async_computation.2 | async-start | bytes 8388608
  1.5 11.6 %slice-start.3 = ((s8[18874368]{0:T(1024)(128)(4,1)}), s8[4194304]{0:T(1024)(128)(4,1)S(1)}, s32[]{:S(2)}) async-start(s8[18874368]{0:T(1024)(128)(4,1)} %bitcast.39), calls=%async_computation.3 | async-start | bytes 8388608
  1.5 11.6 %slice-start.4 = ((s8[18874368]{0:T(1024)(128)(4,1)}), s8[2097152]{0:T(1024)(128)(4,1)S(1)}, s32[]{:S(2)}) async-start(s8[18874368]{0:T(1024)(128)(4,1)} %bitcast.39), calls=%async_computation.4 | async-start | bytes 4194304
  12.7 13.8 %copy-start.9 = (bf16[512,32]{1,0:T(8,128)(2,1)}, bf16[512,32]{1,0:T(8,128)(2,1)S(1)}, u32[]{:S(2)}) copy-start(bf16[512,32]{1,0:T(8,128)(2,1)S(1)} %get-tuple-element.23) | copy-start | bytes 98308
  12.7 13.8 %copy-start.11 = (bf16[512,32]{1,0:T(8,128)(2,1)}, bf16[512,32]{1,0:T(8,128)(2,1)S(1)}, u32[]{:S(2)}) copy-start(bf16[512,32]{1,0:T(8,128)(2,1)S(1)} %get-tuple-element.24) | copy-start | bytes 98308
  12.9 13.6 %copy-start.8 = (bf16[512,512]{1,0:T(8,128)(2,1)}, bf16[512,512]{1,0:T(8,128)(2,1)S(1)}, u32[]{:S(2)}) copy-start(bf16[512,512]{1,0:T(8,128)(2,1)S(1)} %multiply_convert_fusion.1) | copy-start | bytes 1572868
  26.6 3.5 copy-start.13
  30.1 5.6 %copy-start.14 = (s32[512]{0:T(512)S(1)}, s32[512]{0:T(512)}, u32[]{:S(2)}) copy-start(s32[512]{0:T(512)} %param.13) | copy-start | bytes 6148
  32.4 42.2 %copy-start = (bf16[1536,512]{1,0:T(8,128)(2,1)}, bf16[1536,512]{1,0:T(8,128)(2,1)S(1)}, u32[]{:S(2)}) copy-start(bf16[1536,512]{1,0:T(8,128)(2,1)S(1)} %fusion.r_8_) | copy-start | bytes 4718596
  32.4 42.2 %collective-permute-start.3 = (bf16[1536,512]{1,0:T(8,128)(2,1)S(1)}, bf16[1536,512]{1,0:T(8,128)(2,1)}, u32[]{:S(2)}, u32[]{:S(2)}) collective-permute-start(bf16[1536,512]{1,0:T(8,128)(2,1)S(1)} %fusion.r_8_), channel_id=1, source_target_pairs={{0,1},{1,0},{2,3},{3,2},{4,5},{5,4},{6,7},{7,6}} | collective-permute-start | bytes 4718600 | tf_op jit(solution)/shard_map/ppermute | solution.py:180
  33.3 17.9 %collective-permute-start.1 = (bf16[512,640]{1,0:T(8,128)(2,1)S(1)}, bf16[512,640]{1,0:T(8,128)(2,1)S(1)}, u32[]{:S(2)}, u32[]{:S(2)}) collective-permute-start(bf16[512,640]{1,0:T(8,128)(2,1)S(1)} %maximum_maximum_fusion.r_4_), channel_id=1, source_target_pairs={{0,2},{1,3},{2,0},{3,1},{4,6},{5,7},{6,4},{7,5}} | collective-permute-start | bytes 1966088 | tf_op jit(solution)/shard_map/ppermute | solution.py:180
  35.7 2.1 collective-permute-start.4
  35.9 33.6 %collective-permute-start.6 = (s32[512]{0:T(512)S(1)}, s32[512]{0:T(512)}, u32[]{:S(2)}, u32[]{:S(2)}) collective-permute-start(s32[512]{0:T(512)S(1)} %copy-done.14), channel_id=1, source_target_pairs={{0,3},{1,2},{2,1},{3,0},{4,7},{5,6},{6,5},{7,4}} | collective-permute-start | bytes 6152 | tf_op jit(solution)/shard_map/ppermute | solution.py:180
  35.9 34.9 %collective-permute-start.5 = (s32[512]{0:T(512)S(1)}, s32[512]{0:T(512)}, u32[]{:S(2)}, u32[]{:S(2)}) collective-permute-start(s32[512]{0:T(512)S(1)} %copy-done.14), channel_id=1, source_target_pairs={{0,2},{1,3},{2,0},{3,1},{4,6},{5,7},{6,4},{7,5}} | collective-permute-start | bytes 6152 | tf_op jit(solution)/shard_map/ppermute | solution.py:180
  37.9 36.7 %collective-permute-start = (bf16[512,640]{1,0:T(8,128)(2,1)S(1)}, bf16[512,640]{1,0:T(8,128)(2,1)S(1)}, u32[]{:S(2)}, u32[]{:S(2)}) collective-permute-start(bf16[512,640]{1,0:T(8,128)(2,1)S(1)} %maximum_maximum_fusion.r_4_), channel_id=1, source_target_pairs={{0,1},{1,0},{2,3},{3,2},{4,5},{5,4},{6,7},{7,6}} | collective-permute-start | bytes 1966088 | tf_op jit(solution)/shard_map/ppermute | solution.py:180
  51.2 23.5 %copy-start.3 = (bf16[512,640]{1,0:T(8,128)(2,1)}, bf16[512,640]{1,0:T(8,128)(2,1)S(1)}, u32[]{:S(2)}) copy-start(bf16[512,640]{1,0:T(8,128)(2,1)S(1)} %collective-permute-done.1.r_6_) | copy-start | bytes 1966084
  51.2 23.4 %collective-permute-start.2 = (bf16[512,640]{1,0:T(8,128)(2,1)S(1)}, bf16[512,640]{1,0:T(8,128)(2,1)}, u32[]{:S(2)}, u32[]{:S(2)}) collective-permute-start(bf16[512,640]{1,0:T(8,128)(2,1)S(1)} %collective-permute-done.1.r_6_), channel_id=1, source_target_pairs={{0,1},{1,0},{2,3},{3,2},{4,5},{5,4},{6,7},{7,6}} | collective-permute-start | bytes 1966088 | tf_op jit(solution)/shard_map/ppermute | solution.py:180
  59.9 5.9 %copy-start.7 = (bf16[512,32,128]{2,1,0:T(8,128)(2,1)S(1)}, bf16[512,32,128]{2,1,0:T(8,128)(2,1)}, u32[]{:S(2)}) copy-start(bf16[512,32,128]{2,1,0:T(8,128)(2,1)} %get-tuple-element.30) | copy-start | bytes 12582916
  69.6 60.4 %collective-permute-start.8 = (bf16[1536,512]{1,0:T(8,128)(2,1)S(1)}, bf16[1536,512]{1,0:T(8,128)(2,1)S(1)}, u32[]{:S(2)}, u32[]{:S(2)}) collective-permute-start(bf16[1536,512]{1,0:T(8,128)(2,1)S(1)} %fusion.r_8_), channel_id=1, source_target_pairs={{2,1},{3,0},{6,5},{7,4}} | collective-permute-start | bytes 4718600 | tf_op jit(solution)/shard_map/ppermute | solution.py:180
  70.9 71.0 %collective-permute-start.7 = (bf16[1536,512]{1,0:T(8,128)(2,1)S(1)}, bf16[1536,512]{1,0:T(8,128)(2,1)S(1)}, u32[]{:S(2)}, u32[]{:S(2)}) collective-permute-start(bf16[1536,512]{1,0:T(8,128)(2,1)S(1)} %fusion.r_8_), channel_id=1, source_target_pairs={{2,0},{3,1},{6,4},{7,5}} | collective-permute-start | bytes 4718600 | tf_op jit(solution)/shard_map/ppermute | solution.py:180
  74.6 55.3 %copy-start.5 = (bf16[512,640]{1,0:T(8,128)(2,1)}, bf16[512,640]{1,0:T(8,128)(2,1)S(1)}, u32[]{:S(2)}) copy-start(bf16[512,640]{1,0:T(8,128)(2,1)S(1)} %collective-permute-done.r_5_) | copy-start | bytes 1966084
  129.9 11.9 %copy-start.17 = (bf16[1536,512]{1,0:T(8,128)(2,1)}, bf16[1536,512]{1,0:T(8,128)(2,1)S(1)}, u32[]{:S(2)}) copy-start(bf16[1536,512]{1,0:T(8,128)(2,1)S(1)} %collective-permute-done.8.r_11_) | copy-start | bytes 4718596
  141.9 1.2 copy-start.18
  143.0 1.1 copy-start.4
  144.1 1.1 copy-start.6
  145.2 53.3 %copy-start.1 = (bf16[1536,512]{1,0:T(8,128)(2,1)S(1)}, bf16[1536,512]{1,0:T(8,128)(2,1)}, u32[]{:S(2)}) copy-start(bf16[1536,512]{1,0:T(8,128)(2,1)} %copy-done) | copy-start | bytes 4718596
  198.5 59.8 %copy-start.2 = (bf16[512,1024]{1,0:T(8,128)(2,1)}, bf16[512,1024]{1,0:T(8,128)(2,1)S(1)}, u32[]{:S(2)}) copy-start(bf16[512,1024]{1,0:T(8,128)(2,1)S(1)} %get-tuple-element.12.r_11_.b_m) | copy-start | bytes 3145732
  198.5 62.0 %copy-start.10 = (bf16[512,32]{1,0:T(8,128)(2,1)S(1)}, bf16[512,32]{1,0:T(8,128)(2,1)}, u32[]{:S(2)}) copy-start(bf16[512,32]{1,0:T(8,128)(2,1)} %copy-done.9) | copy-start | bytes 98308
  198.5 62.0 %copy-start.12 = (bf16[512,32]{1,0:T(8,128)(2,1)S(1)}, bf16[512,32]{1,0:T(8,128)(2,1)}, u32[]{:S(2)}) copy-start(bf16[512,32]{1,0:T(8,128)(2,1)} %copy-done.11) | copy-start | bytes 98308
  253.6 47.8 %collective-permute-start.11 = (bf16[512,2048]{1,0:T(8,128)(2,1)}, bf16[512,2048]{1,0:T(8,128)(2,1)}, u32[]{:S(2)}, u32[]{:S(2)}) collective-permute-start(bf16[512,2048]{1,0:T(8,128)(2,1)} %get-tuple-element.15), channel_id=1, source_target_pairs={{0,1},{1,0},{2,3},{3,2},{4,5},{5,4},{6,7},{7,6}} | collective-permute-start | bytes 6291464 | tf_op jit(solution)/shard_map/ppermute | solution.py:180
  253.6 47.8 %collective-permute-start.10 = (bf16[512,2048]{1,0:T(8,128)(2,1)}, bf16[512,2048]{1,0:T(8,128)(2,1)}, u32[]{:S(2)}, u32[]{:S(2)}) collective-permute-start(bf16[512,2048]{1,0:T(8,128)(2,1)} %get-tuple-element.14), channel_id=1, source_target_pairs={{0,1},{1,0},{2,3},{3,2},{4,5},{5,4},{6,7},{7,6}} | collective-permute-start | bytes 6291464 | tf_op jit(solution)/shard_map/ppermute | solution.py:180
  254.1 25.1 %collective-permute-start.13 = (bf16[512,1024]{1,0:T(8,128)(2,1)S(1)}, bf16[512,1024]{1,0:T(8,128)(2,1)}, u32[]{:S(2)}, u32[]{:S(2)}) collective-permute-start(bf16[512,1024]{1,0:T(8,128)(2,1)S(1)} %get-tuple-element.16), channel_id=1, source_target_pairs={{0,3},{1,2},{4,7},{5,6}} | collective-permute-start | bytes 3145736 | tf_op jit(solution)/shard_map/ppermute | solution.py:180
  256.6 22.6 %collective-permute-start.12 = (bf16[512,1024]{1,0:T(8,128)(2,1)S(1)}, bf16[512,1024]{1,0:T(8,128)(2,1)}, u32[]{:S(2)}, u32[]{:S(2)}) collective-permute-start(bf16[512,1024]{1,0:T(8,128)(2,1)S(1)} %get-tuple-element.16), channel_id=1, source_target_pairs={{2,3},{3,2},{6,7},{7,6}} | collective-permute-start | bytes 3145736 | tf_op jit(solution)/shard_map/ppermute | solution.py:180
  258.3 43.2 %collective-permute-start.9 = (bf16[512,1024]{1,0:T(8,128)(2,1)S(1)}, bf16[512,1024]{1,0:T(8,128)(2,1)}, u32[]{:S(2)}, u32[]{:S(2)}) collective-permute-start(bf16[512,1024]{1,0:T(8,128)(2,1)S(1)} %get-tuple-element.12.r_11_.b_m), channel_id=1, source_target_pairs={{0,2},{1,3},{4,6},{5,7}} | collective-permute-start | bytes 3145736 | tf_op jit(solution)/shard_map/ppermute | solution.py:180

commit v3 on v2

--- a/solution.py
+++ b/solution.py
@@ -35,7 +35,7 @@
     lats = refs[3:7]
     cqs = refs[7:7 + n_q]
     cs = refs[7 + n_q]
-    o_m, o_o, ckv, cqv, kbuf, vbuf, qbuf, sbuf, m_ref, l_ref, acc, sems = refs[8 + n_q + n_dep:]
+    o_m, o_o, ckv, cqv, kbuf, vbuf, qbuf, sbuf, m_ref, x_ref, l_ref, acc, obuf, sems = refs[8 + n_q + n_dep:]
     me, n_pieces, p_m, p_o, skip, q_slot = (info[k] for k in range(6))
     rows = cqv.shape[2]
     step = pl.program_id(0)
@@ -62,28 +62,6 @@
             for h in range(2):
                 kbuf[h, c, :, 128:] = ckv[c, :, 512:]
 
-    def item(i):
-        st = (i > p_m).astype(jnp.int32)
-        return st, i - st * (p_m + 1)
-
-    def qk(slot, st, c):
-        for h in range(2):
-            sbuf[slot, h] = jnp.dot(kbuf[h, c], qbuf[st, h], preferred_element_type=F32)
-
-    def absorb(slot, st, c, masked):
-        for h in range(2):
-            s = sbuf[slot, h]
-            if masked:
-                keep = lax.broadcasted_iota(jnp.int32, (rows, rows), 0) <= lax.broadcasted_iota(jnp.int32, (rows, rows), 1)
-                s = jnp.where(keep, s, -jnp.inf)
-            m_old = m_ref[st, h]
-            m_new = jnp.maximum(m_old, jnp.max(s, axis=0, keepdims=True))
-            alpha = jnp.exp2((m_old - m_new) * scale)
-            p = jnp.exp2((s - m_new) * scale)
-            m_ref[st, h] = m_new
-            l_ref[st, h] = l_ref[st, h] * alpha + jnp.sum(p.reshape(rows // 8, 8, rows), axis=0)
-            acc[st, h] = acc[st, h] * alpha + jnp.dot(vbuf[c, 128 * h:128 * h + 128], p.astype(BF), preferred_element_type=F32)
-
     @pl.when(step >= skip)
     def _():
         @pl.loop(0, 2)
@@ -107,67 +85,73 @@
             kbuf[1, c, :, :128] = kv[:, 128:256]
             vbuf[c] = kv[:, 256:].T
 
-        m_ref[...] = jnp.full_like(m_ref, -jnp.inf)
-        l_ref[...] = jnp.zeros_like(l_ref)
-        acc[...] = jnp.zeros_like(acc)
-        last = p_m + p_o + 1
-        qk(0, 0, 0)
-
-        @pl.loop(0, last)
-        def _(i):
-            now = jnp.bitwise_and(i, 1)
-            st, c = item(i)
-            st1, c1 = item(i + 1)
-            diag = c == jnp.where(st == 0, p_m, p_o)
-
-            def body(masked):
-                qk(1 - now, st1, c1)
-                absorb(now, st, c, masked)
-
-            @pl.when(diag)
-            def _():
-                body(True)
-
-            @pl.when(jnp.logical_not(diag))
-            def _():
-                body(False)
-
-        absorb(jnp.bitwise_and(last, 1), 1, p_o, True)
+        @pl.loop(0, 2)
+        def _(st):
+            p_st = jnp.where(st == 0, p_m, p_o)
+            m_ref[...] = jnp.full_like(m_ref, -jnp.inf)
+            l_ref[...] = jnp.zeros_like(l_ref)
+            acc[...] = jnp.zeros_like(acc)
+
+            def first(c, h, masked):
+                s = jnp.dot(kbuf[h, c], qbuf[st, h], preferred_element_type=F32)
+                if masked:
+                    keep = lax.broadcasted_iota(jnp.int32, (rows, rows), 0) <= lax.broadcasted_iota(jnp.int32, (rows, rows), 1)
+                    s = jnp.where(keep, s, -jnp.inf)
+                sbuf[c, h] = s
+                m_ref[h] = jnp.maximum(m_ref[h], jnp.max(s.reshape(rows // 8, 8, rows), axis=0))
+
+            def second(c, h):
+                m = x_ref[h]
+                p = jnp.exp2((sbuf[c, h] - m) * scale)
+                l_ref[h] = l_ref[h] + jnp.sum(p.reshape(rows // 8, 8, rows), axis=0)
+                acc[h] = acc[h] + jnp.dot(vbuf[c, pl.ds(128 * h, 128)], p.astype(BF), preferred_element_type=F32)
+
+            def both(f):
+                f(0)
+                f(1)
+
+            @pl.loop(0, p_st)
+            def _(c):
+                both(lambda h: first(c, h, False))
+
+            both(lambda h: first(p_st, h, True))
+            for h in range(2):
+                x_ref[h] = jnp.max(m_ref[h], axis=0, keepdims=True)
+
+            @pl.loop(0, p_st + 1)
+            def _(c):
+                both(lambda h: second(c, h))
+
+            for h in range(2):
+                total = jnp.sum(l_ref[h], axis=0, keepdims=True)
+                obuf[st, h] = (acc[h] * (1.0 / total)).astype(BF).T
+
         for st, out in ((0, o_m), (1, o_o)):
             for h in range(2):
-                total = jnp.sum(l_ref[st, h], axis=0, keepdims=True)
-                out[:, 128 * h:128 * h + 128] = (acc[st, h] * (1.0 / total)).astype(BF).T
-
-
-def out_kernel(info, a_a, a_c, b_m, r_m, s_a, s_c, s_b, r_o, wa, wb, y, buf, sems):
-    late = info[0] >= 2
-    rows, seg = buf.shape[0] // 2, buf.shape[1] // 4
-
-    def cols(ref, k):
-        return ref.at[:, pl.ds(k * seg, seg)]
+                out[:, 128 * h:128 * h + 128] = obuf[st, h]
+
+
+def out_kernel(early, late, info, a_m, c_m, b_m, r_m, a_o, c_o, b_o, r_o, wa, wb, y, buf, sems):
+    col = 256
 
     @pl.when(pl.program_id(0) == 0)
     def _():
-        def plan(is_late):
-            mine = [cols(a_a, 1), b_m if is_late else cols(a_c, 0), cols(a_c, 1), r_m if is_late else cols(a_a, 0)]
-            other = [cols(s_a, 1), s_b if is_late else cols(s_c, 0), cols(s_c, 1), r_o if is_late else cols(s_a, 0)]
-            return [pltpu.make_async_copy(src, buf.at[pl.ds(g * rows, rows), pl.ds(k * seg, seg)], sems.at[4 * g + k])
-                    for g, part in enumerate((mine, other)) for k, src in enumerate(part)]
-
-        for is_late in (False, True):
-            @pl.when(late == is_late)
+        for is_late, runs in ((False, early), (True, late)):
+            @pl.when((info[0] >= 2) == is_late)
             def _():
-                for c in plan(is_late):
+                copies = []
+                for g, part in enumerate(((a_m, b_m, c_m, r_m), (a_o, b_o, c_o, r_o))):
+                    for n, (src, first, count, place) in enumerate(runs):
+                        copies.append(pltpu.make_async_copy(
+                            part[src].at[:, pl.ds(first * col, count * col)],
+                            buf.at[g, :, pl.ds(place * col, count * col)], sems.at[4 * g + n]))
+                for c in copies:
                     c.start()
-        for c in plan(False):
-            c.wait()
-
-    half = rows // 2
-
-    @pl.loop(0, 2)
-    def _(k):
-        r = jnp.dot(buf[pl.ds(k * half, half)], wa[...], preferred_element_type=F32) + jnp.dot(buf[pl.ds(rows + k * half, half)], wb[...], preferred_element_type=F32)
-        y[pl.ds(k * half, half)] = r.astype(BF)
+                for c in copies:
+                    c.wait()
+
+    r = jnp.dot(buf[0], wa[...], preferred_element_type=F32) + jnp.dot(buf[1], wb[...], preferred_element_type=F32)
+    y[...] = r.astype(BF)
 
 
 def solution(mesh):
@@ -188,11 +172,11 @@
         half = rot // 2
         own = heads // 2
         pairs = own // 2
-        moved = 4
+        moved = 3
         scale = (0.1 * math.log(YARN_FACTOR) + 1.0) ** 2 / math.sqrt(qk_dim) * math.log2(math.e)
         me = lax.axis_index('sp')
         core = jnp.bitwise_and(me, 1)
-        late = me >= 2
+        is_late = me >= 2
 
         pos = jnp.stack([tok_pos] + [xor(tok_pos, k) for k in range(1, 4)])
         angles = pos.astype(F32)[:, None, :] * rope_freqs(rot)[None, :, None]
@@ -213,7 +197,7 @@
         c_q = (uq * inv * g_q).astype(BF).T
         cq_o = xor(c_q, 1)
         cq_x = xor(c_q, 2, (2, 3))
-        cq_y = xor(c_q, 3, (2, 3))
+        cq_y = xor(cq_x, 1, (0, 1))
 
         wq_t = jnp.transpose(w_uq, (1, 2, 0)).reshape(heads * qk_dim, q_rank)
         wk_h = jnp.transpose(lax.dynamic_slice_in_dim(w_uk, core * own, own, axis=1), (1, 0, 2))
@@ -222,15 +206,15 @@
         hbm = pl.BlockSpec(memory_space=pl.ANY)
 
         def attend(steps, early_pair, late_pair, late_skip, foreign, *deps):
-            pair0 = jnp.where(late, late_pair, early_pair)
-            skip = jnp.where(late, late_skip, 0)
+            pair0 = jnp.where(is_late, late_pair, early_pair)
+            skip = jnp.where(is_late, late_skip, 0)
             if foreign:
-                base = jnp.where(late, me, me ^ 2)
+                base = jnp.where(is_late, me, me ^ 2)
                 pieces = jnp.full((), 4, jnp.int32)
-                slot = jnp.where(late, 0, 2)
+                slot = jnp.where(is_late, 0, 2)
                 cqs = [c_q, cq_o, cq_x, cq_y]
             else:
-                base, pieces, slot = me, jnp.where(late, 4, 2), jnp.zeros((), jnp.int32)
+                base, pieces, slot = me, jnp.where(is_late, 4, 2), jnp.zeros((), jnp.int32)
                 cqs = [c_q, cq_o]
             info = jnp.stack([me, pieces, base, base ^ 1, skip, slot, pair0, core]).astype(jnp.int32)
 
@@ -254,10 +238,12 @@
                         pltpu.VMEM((2, groups, rows, 256), BF),
                         pltpu.VMEM((groups, 2 * v_dim, rows), BF),
                         pltpu.VMEM((2, 2, 256, rows), BF),
-                        pltpu.VMEM((2, 2, rows, rows), F32),
-                        pltpu.VMEM((2, 2, 1, rows), F32),
-                        pltpu.VMEM((2, 2, 8, rows), F32),
-                        pltpu.VMEM((2, 2, v_dim, rows), F32),
+                        pltpu.VMEM((groups, 2, rows, rows), F32),
+                        pltpu.VMEM((2, 8, rows), F32),
+                        pltpu.VMEM((2, 1, rows), F32),
+                        pltpu.VMEM((2, 8, rows), F32),
+                        pltpu.VMEM((2, v_dim, rows), F32),
+                        pltpu.VMEM((2, 2, rows, v_dim), BF),
                         pltpu.SemaphoreType.DMA((6,)),
                     ],
                 ),
@@ -266,20 +252,22 @@
                 cost_estimate=pl.CostEstimate(flops=5 * steps * 10 ** 9, bytes_accessed=2 * steps << 20, transcendentals=10 ** 7),
             )(info, wq_t, wk_h, wv_h, *lats, *cqs, cs, *deps)
 
-        a_m, a_o = attend(8, pairs - moved, pairs - moved, moved, False)
+        a_m, a_o = attend(6, 10, 7, 2, False)
         s_a = xor(a_o, 1)
-        b_m, b_o = attend(moved, pairs - moved, 4, 0, True, a_m)
+        b_m, b_o = attend(moved, pairs - moved, 6, 0, True, a_m)
         r_m = xor(b_m, 2, (0, 1))
         r_o = xor(b_o, 3, (0, 1))
         s_b = xor(b_o, 1, (2, 3))
-        c_m, c_o = attend(8, 4, 4, moved, False, b_m)
+        c_m, c_o = attend(10, 0, pairs - 4, 4, False, b_m)
         s_c = xor(c_o, 1)
+        early = ((2, 0, 10, 0), (0, 0, 6, 10))
+        late = ((2, 4, 6, 0), (1, 0, 3, 6), (0, 2, 4, 9), (3, 0, 3, 13))
         bn = 512
         depth = own * v_dim
         info = jnp.stack([me, core]).astype(jnp.int32)
         w_o2 = w_o.reshape(heads * v_dim, width)
         attn_out = pl.pallas_call(
-            out_kernel,
+            lambda *r: out_kernel(early, late, *r),
             grid_spec=pltpu.PrefetchScalarGridSpec(
                 num_scalar_prefetch=1,
                 grid=(width // bn,),
@@ -287,7 +275,7 @@
                     pl.BlockSpec((depth, bn), lambda n, i: (i[1], n)),
                     pl.BlockSpec((depth, bn), lambda n, i: (1 - i[1], n))],
                 out_specs=pl.BlockSpec((rows, bn), lambda n, i: (0, n)),
-                scratch_shapes=[pltpu.VMEM((2 * rows, depth), BF), pltpu.SemaphoreType.DMA((8,))],
+                scratch_shapes=[pltpu.VMEM((2, rows, depth), BF), pltpu.SemaphoreType.DMA((8,))],
             ),
             out_shape=jax.ShapeDtypeStruct((rows, width), BF),
             compiler_params=pltpu.CompilerParams(dimension_semantics=("arbitrary",), vmem_limit_bytes=56 << 20),

time: 369 us -> 371 us (level)
  Pallas kernels: 230 us -> 208 us
  starting transfers between devices: 15 us -> 31.8 us
  waiting for transfers between devices: 64.7 us -> 72.6 us
    pallas_call x3, Pallas kernels: 164 us -> 144 us  [attend(): pl.pallas_call(lambda *r: attn_kernel(scale, len(cqs), len(deps), *r), gr...]
    ppermute x14, starting transfers between devices: 15 us -> 31.8 us  [xor(): return lax.ppermute(x, 'sp', [(i, i ^ k) for i in sources])]
    ppermute x14, waiting for transfers between devices: 64.7 us -> 72.6 us  [xor(): return lax.ppermute(x, 'sp', [(i, i ^ k) for i in sources])]
    unnamed x51 -> x47, local copies, waits for them, and re-layouts: 13.7 us -> 13.5 us
  transfers between devices with their start and end apart: 14 -> 14, of which waited for: 4 -> 4; matrix products, arithmetic and copies ran while one was open for 6% -> 6% of each run, Pallas kernels for 15% -> 11%
where the time goes in v3:
time: 371 us
  Pallas kernels  208 us (56%)
  waiting for transfers between devices  72.6 us (20%)
  starting transfers between devices  31.8 us (9%)
  local copies, waits for them, and re-layouts  25.7 us (7%)
  matrix products  23.1 us (6%)
  other arithmetic  7.91 us (2%)
    pallas_call x3, Pallas kernels, attend(): pl.pallas_call(lambda *r: attn_kernel(scale, len(cqs), len(deps), *r), gr...  144 us
    ppermute x14, waiting for transfers between devices, xor(): return lax.ppermute(x, 'sp', [(i, i ^ k) for i in sources])  72.6 us
    pallas_call x1, Pallas kernels, run(): pl.pallas_call(lambda *r: out_kernel(early, late, *r), grid_spec=pltpu.Pr...  64.5 us
    ppermute x14, starting transfers between devices, xor(): return lax.ppermute(x, 'sp', [(i, i ^ k) for i in sources])  31.8 us
    unnamed x47, local copies, waits for them, and re-layouts  13.5 us
    dot_general x1, matrix products, run(): uq = jnp.dot(tok_in, w_dq, preferred_element_type=F32)  13.4 us
    dot_general x1, matrix products, run(): kv = jnp.dot(tok_in, w_dkv, preferred_element_type=F32)  9.73 us
    dynamic_slice x1, local copies, waits for them, and re-layouts, run(): lax.dynamic_slice_in_dim(w_uv, core * own, own, axis=1)  8.37 us
  transfers between devices with their start and end apart: 14, of which 4 were waited for; matrix products, arithmetic and copies ran while one was open for 6% of the time, Pallas kernels for 11%

profile of v3, /device:TPU:0, one launch (start us, length us, event | category | flops | bytes accessed | tf_op | source)
XLA Modules:
  0.0 370.7 jit_solution(1526183648217246768)
XLA Ops:
  0.6 0.0 slice-start
  0.6 0.8 convert_element_type.22
  1.5 0.0 slice-start.3
  1.5 0.0 slice-start.4
  1.5 9.7 %fusion.9 = f32[512,576]{1,0:T(8,128)S(1)} fusion(bf16[512,6144]{1,0:T(8,128)(2,1)} %param.12, bf16[6144,576]{0,1:T(8,128)(2,1)} %param.17), kind=kOutput, calls=%fused_computation.28 | convolution fusion | flops 3623878656 | bytes 14548992 | tf_op jit(solution)/shard_map/dot_general | solution.py:186
  11.2 0.1 multiply_reduce_fusion.1
  11.4 0.1 pad.11.clone
  11.5 0.0 copy-done.16
  11.5 1.2 fusion.6
  12.7 0.0 copy-done.14
  12.7 0.2 multiply_convert_fusion.1
  12.9 0.0 copy-start.5
  12.9 0.4 copy-done.7
  13.4 0.1 copy-done.9
  13.4 0.3 copy-done.5
  13.7 0.2 maximum_maximum_fusion.r_4_
  13.9 13.4 %multiply_reduce_fusion = (f32[512]{0:T(512)S(1)}, f32[512,1536]{1,0:T(8,128)}) fusion(bf16[512,6144]{1,0:T(8,128)(2,1)} %param.12, bf16[6144,1536]{1,0:T(8,128)(2,1)S(1)} %bitcast.44), kind=kOutput, calls=%fused_computation.3 | convolution fusion | flops 9665249280 | bytes 28313600 | tf_op jit(solution)/shard_map/dot_general | solution.py:195
  27.4 3.5 copy.28
  30.9 2.2 fusion.r_8_
  33.2 1.5 collective-permute-start.7
  34.6 0.9 collective-permute-start.3
  35.5 3.4 collective-permute-start.1
  38.9 0.2 collective-permute-start.4
  39.2 0.0 collective-permute-start.6
  39.2 0.9 collective-permute-done.4
  40.1 2.4 collective-permute-start.5
  42.5 43.1 %collective-permute-done.6 = s32[512]{0:T(512)} collective-permute-done((s32[512]{0:T(512)S(1)}, s32[512]{0:T(512)}, u32[]{:S(2)}, u32[]{:S(2)}) %collective-permute-start.6) | collective-permute-done | bytes 2080 | tf_op jit(solution)/shard_map/ppermute | solution.py:164
  85.6 0.8 collective-permute-start
  86.4 0.0 collective-permute-done.1.r_6_
  86.4 0.0 collective-permute-start.2
  86.4 8.4 %constant_dynamic-slice_fusion = (bf16[512,32,128]{2,1,0:T(8,128)(2,1)}, bf16[512,32,128]{2,1,0:T(8,128)(2,1)}) fusion(bf16[512,64,128]{2,1,0:T(8,128)(2,1)} %param.20, s32[]{:T(128)S(6)} %select_n.35, bf16[512,64,128]{2,1,0:T(8,128)(2,1)} %param.19), kind=kLoop, calls=%fused_computation.26 | loop fusion | bytes 16777220 | tf_op jit(solution)/shard_map/dynamic_slice | solution.py:204
  94.8 5.9 %copy.35 = bf16[512,32,128]{2,0,1:T(8,128)(2,1)} copy(bf16[512,32,128]{2,1,0:T(8,128)(2,1)} %get-tuple-element.29) | data formatting | bytes 8388608
  100.7 3.6 copy.36
  104.4 0.1 stack.89.r_0_
  104.4 0.1 stack.81.r_0_
  104.5 0.1 stack.94.r_0_
  104.6 0.0 collective-permute-done.5
  104.6 0.7 add_convert_fusion
  105.3 1.6 multiply_cosine_fusion
  107.0 0.0 collective-permute-done.7.r_10_
  107.0 2.6 collective-permute-start.8
  109.7 0.0 collective-permute-done.r_5_
  109.7 0.0 collective-permute-done.2.r_7_
  109.7 0.0 collective-permute-done.3.r_9_
  109.7 41.3 %shard_map.139 = (bf16[512,1536]{1,0:T(8,128)(2,1)S(1)}, bf16[512,1536]{1,0:T(8,128)(2,1)}) custom-call(s32[8]{0:T(128)S(1)} %stack.81.r_0_, bf16[12288,1536]{1,0:T(8,128)(2,1)} %bitcast.32, bf16[32,512,128]{2,1,0:T(8,128)(2,1)} %bitcast.38, bf16[32,512,128]{2,1,0:T(8,128)(2,1)} %bitcast.35, bf16[512,640]{1,0:T(8,128)(2,1)S(1)} %maximum_maximum_fusion.r_4_, ...), custom_call_target="tpu_custom_call" | custom-call | flops 30000001024 | bytes 12582912 | tf_op jit(solution)/shard_map/pallas_call | solution.py:224
  151.0 1.2 copy-done
  152.2 0.0 collective-permute-done.8.r_11_
  152.2 1.2 copy-done.6
  153.4 37.1 %shard_map.140 = (bf16[512,768]{1,0:T(8,128)(2,1)S(1)}, bf16[512,768]{1,0:T(8,128)(2,1)S(1)}) custom-call(s32[8]{0:T(128)S(1)} %stack.94.r_0_, bf16[12288,1536]{1,0:T(8,128)(2,1)} %bitcast.33, bf16[32,512,128]{2,1,0:T(8,128)(2,1)} %bitcast.39, bf16[32,512,128]{2,1,0:T(8,128)(2,1)} %bitcast.36, bf16[512,640]{1,0:T(8,128)(2,1)S(1)} %maximum_maximum_fusion.r_4_, ...), custom_call_target="tpu_custom_call" | custom-call | flops 15000000512 | bytes 6291456 | tf_op jit(solution)/shard_map/pallas_call | solution.py:224
  190.5 65.3 %shard_map.141 = (bf16[512,2560]{1,0:T(8,128)(2,1)}, bf16[512,2560]{1,0:T(8,128)(2,1)}) custom-call(s32[8]{0:T(128)S(1)} %stack.89.r_0_, bf16[12288,1536]{1,0:T(8,128)(2,1)} %bitcast.34, bf16[32,512,128]{2,1,0:T(8,128)(2,1)} %bitcast.40, bf16[32,512,128]{2,1,0:T(8,128)(2,1)} %bitcast.37, bf16[512,640]{1,0:T(8,128)(2,1)S(1)} %maximum_maximum_fusion.r_4_, ...), custom_call_target="tpu_custom_call" | custom-call | flops 49999998976 | bytes 20971520 | tf_op jit(solution)/shard_map/pallas_call | solution.py:224
  255.9 0.0 collective-permute-start.11
  255.9 0.5 collective-permute-start.10
  256.4 15.0 %collective-permute-start.13 = (bf16[512,768]{1,0:T(8,128)(2,1)S(1)}, bf16[512,768]{1,0:T(8,128)(2,1)S(1)}, u32[]{:S(2)}, u32[]{:S(2)}) collective-permute-start(bf16[512,768]{1,0:T(8,128)(2,1)S(1)} %get-tuple-element.16), channel_id=1, source_target_pairs={{0,3},{1,2},{4,7},{5,6}} | collective-permute-start | bytes 2359304 | tf_op jit(solution)/shard_map/ppermute | solution.py:164
  271.4 1.6 collective-permute-start.12
  273.0 2.9 collective-permute-start.9
  275.9 0.1 pad_maximum_fusion.1
  276.0 0.7 copy.29
  276.8 0.6 pad_add_fusion.r_0_
  277.4 0.0 collective-permute-done.10.r_5_
  277.4 11.9 %collective-permute-done.13.r_8_ = bf16[512,768]{1,0:T(8,128)(2,1)S(1)} collective-permute-done((bf16[512,768]{1,0:T(8,128)(2,1)S(1)}, bf16[512,768]{1,0:T(8,128)(2,1)S(1)}, u32[]{:S(2)}, u32[]{:S(2)}) %collective-permute-start.13) | collective-permute-done | bytes 786464 | tf_op jit(solution)/shard_map/ppermute | solution.py:164
  289.3 0.0 collective-permute-done.12.r_7_
  289.3 16.6 %collective-permute-done.9.r_4_ = bf16[512,768]{1,0:T(8,128)(2,1)} collective-permute-done((bf16[512,768]{1,0:T(8,128)(2,1)S(1)}, bf16[512,768]{1,0:T(8,128)(2,1)}, u32[]{:S(2)}, u32[]{:S(2)}) %collective-permute-start.9) | collective-permute-done | bytes 786464 | tf_op jit(solution)/shard_map/ppermute | solution.py:164
  306.0 0.0 collective-permute-done.11.r_6_
  306.0 64.5 %outproj.1 = bf16[512,6144]{1,0:T(8,128)(2,1)} custom-call(s32[2]{0:T(128)} %pad_add_fusion.r_0_, bf16[512,1536]{1,0:T(8,128)(2,1)} %copy-done, bf16[512,2560]{1,0:T(8,128)(2,1)} %get-tuple-element.13.r_2_, bf16[512,768]{1,0:T(8,128)(2,1)} %copy-done.3, bf16[512,768]{1,0:T(8,128)(2,1)} %collective-permute-done.9.r_4_, ...), custom_call_target="tpu_custom_call" | custom-call | flops 51999997952 | bytes 115343360 | tf_op jit(solution)/shard_map/outproj/pallas_call | solution.py:269
  (38 shorter events, 0.1 us)
Async XLA Ops:
  0.6 13.3 %slice-start = ((s8[18874368]{0:T(1024)(128)(4,1)}), s8[4194304]{0:T(1024)(128)(4,1)S(1)}, s32[]{:S(2)}) async-start(s8[18874368]{0:T(1024)(128)(4,1)} %bitcast.43), calls=%async_computation | async-start | bytes 8388608
  1.5 10.0 %copy-start.16 = (f32[32]{0:T(128)S(1)}, f32[32]{0:T(128)}, u32[]{:S(2)}) copy-start(f32[32]{0:T(128)} %constant.45.clone) | copy-start | bytes 388
  1.5 11.2 %copy-start.14 = (f32[512]{0:T(512)S(1)}, f32[512]{0:T(512)}, u32[]{:S(2)}) copy-start(f32[512]{0:T(512)} %param.18) | copy-start | bytes 6148
  1.5 12.4 %slice-start.1 = ((s8[18874368]{0:T(1024)(128)(4,1)}), s8[4194304]{0:T(1024)(128)(4,1)S(1)}, s32[]{:S(2)}) async-start(s8[18874368]{0:T(1024)(128)(4,1)} %bitcast.43), calls=%async_computation.1 | async-start | bytes 8388608
  1.5 12.4 %slice-start.2 = ((s8[18874368]{0:T(1024)(128)(4,1)}), s8[4194304]{0:T(1024)(128)(4,1)S(1)}, s32[]{:S(2)}) async-start(s8[18874368]{0:T(1024)(128)(4,1)} %bitcast.43), calls=%async_computation.2 | async-start | bytes 8388608
  1.5 12.4 %slice-start.3 = ((s8[18874368]{0:T(1024)(128)(4,1)}), s8[4194304]{0:T(1024)(128)(4,1)S(1)}, s32[]{:S(2)}) async-start(s8[18874368]{0:T(1024)(128)(4,1)} %bitcast.43), calls=%async_computation.3 | async-start | bytes 8388608
  1.5 12.4 %slice-start.4 = ((s8[18874368]{0:T(1024)(128)(4,1)}), s8[2097152]{0:T(1024)(128)(4,1)S(1)}, s32[]{:S(2)}) async-start(s8[18874368]{0:T(1024)(128)(4,1)} %bitcast.43), calls=%async_computation.4 | async-start | bytes 4194304
  12.7 0.6 copy-start.7
  12.7 0.7 copy-start.9
  12.9 0.8 copy-start.5
  27.3 3.6 copy-start.12
  30.9 8.0 %copy-start.13 = (s32[512]{0:T(512)S(1)}, s32[512]{0:T(512)}, u32[]{:S(2)}) copy-start(s32[512]{0:T(512)} %param.13) | copy-start | bytes 6148
  33.2 61.6 %copy-start.1 = (bf16[1536,512]{1,0:T(8,128)(2,1)}, bf16[1536,512]{1,0:T(8,128)(2,1)S(1)}, u32[]{:S(2)}) copy-start(bf16[1536,512]{1,0:T(8,128)(2,1)S(1)} %fusion.r_8_) | copy-start | bytes 4718596
  33.2 73.9 %collective-permute-start.7 = (bf16[1536,512]{1,0:T(8,128)(2,1)S(1)}, bf16[1536,512]{1,0:T(8,128)(2,1)}, u32[]{:S(2)}, u32[]{:S(2)}) collective-permute-start(bf16[1536,512]{1,0:T(8,128)(2,1)S(1)} %fusion.r_8_), channel_id=1, source_target_pairs={{2,0},{3,1},{6,4},{7,5}} | collective-permute-start | bytes 4718600 | tf_op jit(solution)/shard_map/ppermute | solution.py:164
  34.6 75.1 %collective-permute-start.3 = (bf16[1536,512]{1,0:T(8,128)(2,1)S(1)}, bf16[1536,512]{1,0:T(8,128)(2,1)}, u32[]{:S(2)}, u32[]{:S(2)}) collective-permute-start(bf16[1536,512]{1,0:T(8,128)(2,1)S(1)} %fusion.r_8_), channel_id=1, source_target_pairs={{0,1},{1,0},{2,3},{3,2},{4,5},{5,4},{6,7},{7,6}} | collective-permute-start | bytes 4718600 | tf_op jit(solution)/shard_map/ppermute | solution.py:164
  35.5 50.9 %collective-permute-start.1 = (bf16[512,640]{1,0:T(8,128)(2,1)S(1)}, bf16[512,640]{1,0:T(8,128)(2,1)S(1)}, u32[]{:S(2)}, u32[]{:S(2)}) collective-permute-start(bf16[512,640]{1,0:T(8,128)(2,1)S(1)} %maximum_maximum_fusion.r_4_), channel_id=1, source_target_pairs={{0,2},{1,3},{2,0},{3,1},{4,6},{5,7},{6,4},{7,5}} | collective-permute-start | bytes 1966088 | tf_op jit(solution)/shard_map/ppermute | solution.py:164
  38.9 1.2 collective-permute-start.4
  39.2 46.4 %collective-permute-start.6 = (s32[512]{0:T(512)S(1)}, s32[512]{0:T(512)}, u32[]{:S(2)}, u32[]{:S(2)}) collective-permute-start(s32[512]{0:T(512)S(1)} %copy-done.13), channel_id=1, source_target_pairs={{0,3},{1,2},{2,1},{3,0},{4,7},{5,6},{6,5},{7,4}} | collective-permute-start | bytes 6152 | tf_op jit(solution)/shard_map/ppermute | solution.py:164
  40.1 2.4 copy-start.15
  40.1 64.5 %collective-permute-start.5 = (s32[512]{0:T(512)S(1)}, s32[512]{0:T(512)}, u32[]{:S(2)}, u32[]{:S(2)}) collective-permute-start(s32[512]{0:T(512)S(1)} %copy-done.13), channel_id=1, source_target_pairs={{0,2},{1,3},{2,0},{3,1},{4,6},{5,7},{6,4},{7,5}} | collective-permute-start | bytes 6152 | tf_op jit(solution)/shard_map/ppermute | solution.py:164
  85.6 24.1 %collective-permute-start = (bf16[512,640]{1,0:T(8,128)(2,1)S(1)}, bf16[512,640]{1,0:T(8,128)(2,1)S(1)}, u32[]{:S(2)}, u32[]{:S(2)}) collective-permute-start(bf16[512,640]{1,0:T(8,128)(2,1)S(1)} %maximum_maximum_fusion.r_4_), channel_id=1, source_target_pairs={{0,1},{1,0},{2,3},{3,2},{4,5},{5,4},{6,7},{7,6}} | collective-permute-start | bytes 1966088 | tf_op jit(solution)/shard_map/ppermute | solution.py:164
  86.4 23.3 %collective-permute-start.2 = (bf16[512,640]{1,0:T(8,128)(2,1)S(1)}, bf16[512,640]{1,0:T(8,128)(2,1)}, u32[]{:S(2)}, u32[]{:S(2)}) collective-permute-start(bf16[512,640]{1,0:T(8,128)(2,1)S(1)} %collective-permute-done.1.r_6_), channel_id=1, source_target_pairs={{0,1},{1,0},{2,3},{3,2},{4,5},{5,4},{6,7},{7,6}} | collective-permute-start | bytes 1966088 | tf_op jit(solution)/shard_map/ppermute | solution.py:164
  94.8 6.0 %copy-start.4 = (bf16[512,32,128]{2,1,0:T(8,128)(2,1)S(1)}, bf16[512,32,128]{2,1,0:T(8,128)(2,1)}, u32[]{:S(2)}) copy-start(bf16[512,32,128]{2,1,0:T(8,128)(2,1)} %get-tuple-element.30) | copy-start | bytes 12582916
  107.0 45.1 %collective-permute-start.8 = (bf16[1536,512]{1,0:T(8,128)(2,1)}, bf16[1536,512]{1,0:T(8,128)(2,1)S(1)}, u32[]{:S(2)}, u32[]{:S(2)}) collective-permute-start(bf16[1536,512]{1,0:T(8,128)(2,1)} %collective-permute-done.7.r_10_), channel_id=1, source_target_pairs={{0,1},{1,0},{4,5},{5,4}} | collective-permute-start | bytes 4718600 | tf_op jit(solution)/shard_map/ppermute | solution.py:164
  151.0 1.2 copy-start
  152.2 1.2 copy-start.6
  153.4 37.2 %copy-start.2 = (bf16[1536,512]{1,0:T(8,128)(2,1)S(1)}, bf16[1536,512]{1,0:T(8,128)(2,1)}, u32[]{:S(2)}) copy-start(bf16[1536,512]{1,0:T(8,128)(2,1)} %copy-done.1) | copy-start | bytes 4718596
  190.5 82.5 %copy-start.3 = (bf16[512,768]{1,0:T(8,128)(2,1)}, bf16[512,768]{1,0:T(8,128)(2,1)S(1)}, u32[]{:S(2)}) copy-start(bf16[512,768]{1,0:T(8,128)(2,1)S(1)} %get-tuple-element.12.r_11_.r_3_) | copy-start | bytes 2359300
  190.5 85.4 %copy-start.8 = (bf16[512,32]{1,0:T(8,128)(2,1)S(1)}, bf16[512,32]{1,0:T(8,128)(2,1)}, u32[]{:S(2)}) copy-start(bf16[512,32]{1,0:T(8,128)(2,1)} %copy-done.7) | copy-start | bytes 98308
  190.5 85.4 %copy-start.10 = (bf16[512,32]{1,0:T(8,128)(2,1)S(1)}, bf16[512,32]{1,0:T(8,128)(2,1)}, u32[]{:S(2)}) copy-start(bf16[512,32]{1,0:T(8,128)(2,1)} %copy-done.9) | copy-start | bytes 98308
  255.9 50.1 %collective-permute-start.11 = (bf16[512,2560]{1,0:T(8,128)(2,1)}, bf16[512,2560]{1,0:T(8,128)(2,1)}, u32[]{:S(2)}, u32[]{:S(2)}) collective-permute-start(bf16[512,2560]{1,0:T(8,128)(2,1)} %get-tuple-element.15), channel_id=1, source_target_pairs={{0,1},{1,0},{2,3},{3,2},{4,5},{5,4},{6,7},{7,6}} | collective-permute-start | bytes 7864328 | tf_op jit(solution)/shard_map/ppermute | solution.py:164
  255.9 21.5 %collective-permute-start.10 = (bf16[512,1536]{1,0:T(8,128)(2,1)}, bf16[512,1536]{1,0:T(8,128)(2,1)}, u32[]{:S(2)}, u32[]{:S(2)}) collective-permute-start(bf16[512,1536]{1,0:T(8,128)(2,1)} %get-tuple-element.14), channel_id=1, source_target_pairs={{0,1},{1,0},{2,3},{3,2},{4,5},{5,4},{6,7},{7,6}} | collective-permute-start | bytes 4718600 | tf_op jit(solution)/shard_map/ppermute | solution.py:164
  256.4 32.9 %collective-permute-start.13 = (bf16[512,768]{1,0:T(8,128)(2,1)S(1)}, bf16[512,768]{1,0:T(8,128)(2,1)S(1)}, u32[]{:S(2)}, u32[]{:S(2)}) collective-permute-start(bf16[512,768]{1,0:T(8,128)(2,1)S(1)} %get-tuple-element.16), channel_id=1, source_target_pairs={{0,3},{1,2},{4,7},{5,6}} | collective-permute-start | bytes 2359304 | tf_op jit(solution)/shard_map/ppermute | solution.py:164
  271.4 17.9 %collective-permute-start.12 = (bf16[512,768]{1,0:T(8,128)(2,1)S(1)}, bf16[512,768]{1,0:T(8,128)(2,1)}, u32[]{:S(2)}, u32[]{:S(2)}) collective-permute-start(bf16[512,768]{1,0:T(8,128)(2,1)S(1)} %get-tuple-element.16), channel_id=1, source_target_pairs={{2,3},{3,2},{6,7},{7,6}} | collective-permute-start | bytes 2359304 | tf_op jit(solution)/shard_map/ppermute | solution.py:164
  273.0 32.9 %collective-permute-start.9 = (bf16[512,768]{1,0:T(8,128)(2,1)S(1)}, bf16[512,768]{1,0:T(8,128)(2,1)}, u32[]{:S(2)}, u32[]{:S(2)}) collective-permute-start(bf16[512,768]{1,0:T(8,128)(2,1)S(1)} %get-tuple-element.12.r_11_.r_3_), channel_id=1, source_target_pairs={{0,2},{1,3},{4,6},{5,7}} | collective-permute-start | bytes 2359304 | tf_op jit(solution)/shard_map/ppermute | solution.py:164
  289.3 16.6 %copy-start.11 = (bf16[512,768]{1,0:T(8,128)(2,1)}, bf16[512,768]{1,0:T(8,128)(2,1)S(1)}, u32[]{:S(2)}) copy-start(bf16[512,768]{1,0:T(8,128)(2,1)S(1)} %collective-permute-done.13.r_8_) | copy-start | bytes 2359300

commit v4 on v3

--- a/solution.py
+++ b/solution.py
@@ -129,6 +129,11 @@
         for st, out in ((0, o_m), (1, o_o)):
             for h in range(2):
                 out[:, 128 * h:128 * h + 128] = obuf[st, h]
+
+
+def head_major(info, a, b, out_a, out_b):
+    out_a[...] = jnp.swapaxes(a[...], 0, 1)
+    out_b[...] = jnp.swapaxes(b[...], 0, 1)
 
 
 def out_kernel(early, late, info, a_m, c_m, b_m, r_m, a_o, c_o, b_o, r_o, wa, wb, y, buf, sems):
@@ -200,8 +205,20 @@
         cq_y = xor(cq_x, 1, (0, 1))
 
         wq_t = jnp.transpose(w_uq, (1, 2, 0)).reshape(heads * qk_dim, q_rank)
-        wk_h = jnp.transpose(lax.dynamic_slice_in_dim(w_uk, core * own, own, axis=1), (1, 0, 2))
-        wv_h = jnp.transpose(lax.dynamic_slice_in_dim(w_uv, core * own, own, axis=1), (1, 0, 2))
+        blocks = own // 8
+        wk_h, wv_h = pl.pallas_call(
+            head_major,
+            grid_spec=pltpu.PrefetchScalarGridSpec(
+                num_scalar_prefetch=1,
+                grid=(blocks,),
+                in_specs=[pl.BlockSpec((kv_rank, 8, v_dim), lambda g, i: (0, i[0] * blocks + g, 0))] * 2,
+                out_specs=[pl.BlockSpec((8, kv_rank, v_dim), lambda g, i: (g, 0, 0))] * 2,
+            ),
+            out_shape=[jax.ShapeDtypeStruct((own, kv_rank, v_dim), BF)] * 2,
+            compiler_params=pltpu.CompilerParams(dimension_semantics=("arbitrary",), vmem_limit_bytes=32 << 20),
+            cost_estimate=pl.CostEstimate(flops=10 ** 8, bytes_accessed=16 << 20, transcendentals=0),
+            name="headmajor",
+        )(core[None], w_uk, w_uv)
         full = pl.BlockSpec(memory_space=pltpu.VMEM)
         hbm = pl.BlockSpec(memory_space=pl.ANY)
 

time: 371 us -> 373 us (level)
  local copies, waits for them, and re-layouts: 25.7 us -> 15.9 us
  waiting for transfers between devices: 72.6 us -> 80.4 us
  Pallas kernels: 208 us -> 213 us
    dynamic_slice x1 -> x0, local copies, waits for them, and re-layouts: 8.37 us -> none  [run(): lax.dynamic_slice_in_dim(w_uv, core * own, own, axis=1)]
    ppermute x14, waiting for transfers between devices: 72.6 us -> 80.4 us  [xor(): return lax.ppermute(x, 'sp', [(i, i ^ k) for i in sources])]
    pallas_call x0 -> x1, Pallas kernels: none -> 4.62 us  [run(): pl.pallas_call(head_major, grid_spec=pltpu.PrefetchScalarGridSpec(num_sca...]
    unnamed x47 -> x51, local copies, waits for them, and re-layouts: 13.5 us -> 12 us
  transfers between devices with their start and end apart: 14 -> 14, of which waited for: 4 -> 5; matrix products, arithmetic and copies ran while one was open for 6% -> 1% of each run, Pallas kernels for 11% -> 12%
where the time goes in v4:
time: 373 us
  Pallas kernels  213 us (57%)
  waiting for transfers between devices  80.4 us (22%)
  starting transfers between devices  31.3 us (8%)
  matrix products  23.1 us (6%)
  local copies, waits for them, and re-layouts  15.9 us (4%)
  other arithmetic  7.92 us (2%)
    pallas_call x3, Pallas kernels, attend(): pl.pallas_call(lambda *r: attn_kernel(scale, len(cqs), len(deps), *r), gr...  144 us
    ppermute x14, waiting for transfers between devices, xor(): return lax.ppermute(x, 'sp', [(i, i ^ k) for i in sources])  80.4 us
    pallas_call x1, Pallas kernels, run(): pl.pallas_call(lambda *r: out_kernel(early, late, *r), grid_spec=pltpu.Pr...  64.5 us
    ppermute x14, starting transfers between devices, xor(): return lax.ppermute(x, 'sp', [(i, i ^ k) for i in sources])  31.3 us
    dot_general x1, matrix products, run(): uq = jnp.dot(tok_in, w_dq, preferred_element_type=F32)  13.4 us
    unnamed x51, local copies, waits for them, and re-layouts  12 us
    dot_general x1, matrix products, run(): kv = jnp.dot(tok_in, w_dkv, preferred_element_type=F32)  9.73 us
  transfers between devices with their start and end apart: 14, of which 5 were waited for; matrix products, arithmetic and copies ran while one was open for 1% of the time, Pallas kernels for 12%

profile of v4, /device:TPU:0, one launch (start us, length us, event | category | flops | bytes accessed | tf_op | source)
XLA Modules:
  0.0 372.6 jit_solution(13378165717570388863)
XLA Ops:
  0.6 0.0 slice-start
  0.6 0.8 convert_element_type.22
  1.5 0.0 slice-start.3
  1.5 0.0 slice-start.4
  1.5 9.7 %fusion.9 = f32[512,576]{1,0:T(8,128)S(1)} fusion(bf16[512,6144]{1,0:T(8,128)(2,1)} %param.12, bf16[6144,576]{0,1:T(8,128)(2,1)} %param.17), kind=kOutput, calls=%fused_computation.24 | convolution fusion | flops 3623878656 | bytes 14548992 | tf_op jit(solution)/shard_map/dot_general | solution.py:191
  11.2 0.1 multiply_reduce_fusion.1
  11.4 0.1 pad.11.clone
  11.5 1.2 fusion.6
  12.7 0.2 multiply_convert_fusion.1
  12.9 0.0 copy-start.7
  12.9 0.5 copy-done.9
  13.4 0.1 copy-done.11
  13.4 0.3 copy-done.7
  13.7 0.2 maximum_maximum_fusion.r_4_
  13.9 13.4 %multiply_reduce_fusion = (f32[512]{0:T(512)S(1)}, f32[512,1536]{1,0:T(8,128)}) fusion(bf16[512,6144]{1,0:T(8,128)(2,1)} %param.12, bf16[6144,1536]{1,0:T(8,128)(2,1)S(1)} %bitcast.33), kind=kOutput, calls=%fused_computation.1 | convolution fusion | flops 9665249280 | bytes 28313600 | tf_op jit(solution)/shard_map/dot_general | solution.py:200
  27.4 3.6 copy.24
  30.9 2.2 fusion.r_8_
  33.2 1.3 collective-permute-start.7
  34.5 0.9 collective-permute-start.3
  35.3 3.6 collective-permute-start.1
  38.9 0.2 collective-permute-start
  39.2 47.1 %collective-permute-done.1.r_6_ = bf16[512,640]{1,0:T(8,128)(2,1)S(1)} collective-permute-done((bf16[512,640]{1,0:T(8,128)(2,1)S(1)}, bf16[512,640]{1,0:T(8,128)(2,1)S(1)}, u32[]{:S(2)}, u32[]{:S(2)}) %collective-permute-start.1) | collective-permute-done | bytes 655392 | tf_op jit(solution)/shard_map/ppermute | solution.py:169
  86.2 0.0 collective-permute-start.2
  86.3 0.5 collective-permute-start.4
  86.8 1.7 collective-permute-done.4
  88.5 0.6 copy-done.17
  89.0 0.0 collective-permute-start.6
  89.1 3.0 collective-permute-done.6
  92.1 0.1 collective-permute-start.5
  92.1 3.4 copy-done
  95.5 4.6 %headmajor.1 = (bf16[32,512,128]{2,1,0:T(8,128)(2,1)S(1)}, bf16[32,512,128]{2,1,0:T(8,128)(2,1)S(1)}) custom-call(s32[1]{0:T(128)} %bitcast.1.info, bf16[512,64,128]{2,1,0:T(8,128)(2,1)S(1)} %copy-done, bf16[512,64,128]{2,1,0:T(8,128)(2,1)} %b.1), custom_call_target="tpu_custom_call" | custom-call | flops 100000000 | bytes 16777216 | tf_op jit(solution)/shard_map/headmajor/pallas_call | solution.py:209
  100.2 0.0 copy-start.4
  100.2 2.0 copy-done.4
  102.2 2.0 copy-done.5
  104.1 0.1 stack.89.r_0_
  104.2 0.1 stack.81.r_0_
  104.3 0.1 stack.94.r_0_
  104.4 0.0 collective-permute-done.5
  104.4 0.7 add_convert_fusion
  105.1 1.6 multiply_cosine_fusion
  106.8 0.0 collective-permute-done.7.r_10_
  106.8 2.2 collective-permute-start.8
  109.0 0.0 collective-permute-done.r_5_
  109.0 0.0 collective-permute-done.2.r_7_
  109.0 0.0 collective-permute-done.3.r_9_
  109.0 41.3 %shard_map.139 = (bf16[512,1536]{1,0:T(8,128)(2,1)S(1)}, bf16[512,1536]{1,0:T(8,128)(2,1)}) custom-call(s32[8]{0:T(128)S(1)} %stack.81.r_0_, bf16[12288,1536]{1,0:T(8,128)(2,1)} %bitcast.26, bf16[32,512,128]{2,1,0:T(8,128)(2,1)} %copy-done.4, bf16[32,512,128]{2,1,0:T(8,128)(2,1)} %copy-done.5, bf16[512,640]{1,0:T(8,128)(2,1)S(1)} %maximum_maximum_fusion.r_4_, ...), custom_call_target="tpu_custom_call" | custom-call | flops 30000001024 | bytes 12582912 | tf_op jit(solution)/shard_map/pallas_call | solution.py:241
  150.3 1.2 copy-done.1
  151.5 0.0 collective-permute-done.8.r_11_
  151.5 1.3 copy-done.8
  152.8 37.1 %shard_map.140 = (bf16[512,768]{1,0:T(8,128)(2,1)S(1)}, bf16[512,768]{1,0:T(8,128)(2,1)S(1)}) custom-call(s32[8]{0:T(128)S(1)} %stack.94.r_0_, bf16[12288,1536]{1,0:T(8,128)(2,1)} %bitcast.27, bf16[32,512,128]{2,1,0:T(8,128)(2,1)} %copy-done.4, bf16[32,512,128]{2,1,0:T(8,128)(2,1)} %copy-done.5, bf16[512,640]{1,0:T(8,128)(2,1)S(1)} %maximum_maximum_fusion.r_4_, ...), custom_call_target="tpu_custom_call" | custom-call | flops 15000000512 | bytes 6291456 | tf_op jit(solution)/shard_map/pallas_call | solution.py:241
  190.0 65.3 %shard_map.141 = (bf16[512,2560]{1,0:T(8,128)(2,1)}, bf16[512,2560]{1,0:T(8,128)(2,1)}) custom-call(s32[8]{0:T(128)S(1)} %stack.89.r_0_, bf16[12288,1536]{1,0:T(8,128)(2,1)} %bitcast.28, bf16[32,512,128]{2,1,0:T(8,128)(2,1)} %copy-done.4, bf16[32,512,128]{2,1,0:T(8,128)(2,1)} %copy-done.5, bf16[512,640]{1,0:T(8,128)(2,1)S(1)} %maximum_maximum_fusion.r_4_, ...), custom_call_target="tpu_custom_call" | custom-call | flops 49999998976 | bytes 20971520 | tf_op jit(solution)/shard_map/pallas_call | solution.py:241
  255.3 0.4 collective-permute-start.11
  255.8 0.1 collective-permute-start.10
  255.9 17.6 %collective-permute-start.13 = (bf16[512,768]{1,0:T(8,128)(2,1)S(1)}, bf16[512,768]{1,0:T(8,128)(2,1)S(1)}, u32[]{:S(2)}, u32[]{:S(2)}) collective-permute-start(bf16[512,768]{1,0:T(8,128)(2,1)S(1)} %get-tuple-element.20), channel_id=1, source_target_pairs={{0,3},{1,2},{4,7},{5,6}} | collective-permute-start | bytes 2359304 | tf_op jit(solution)/shard_map/ppermute | solution.py:169
  273.4 1.6 collective-permute-start.12
  275.0 2.9 collective-permute-start.9
  277.9 0.1 pad_maximum_fusion.1
  278.0 0.7 copy.25
  278.7 0.6 pad_add_fusion.r_0_
  279.4 0.0 collective-permute-done.10.r_5_
  279.4 11.9 %collective-permute-done.13.r_8_ = bf16[512,768]{1,0:T(8,128)(2,1)S(1)} collective-permute-done((bf16[512,768]{1,0:T(8,128)(2,1)S(1)}, bf16[512,768]{1,0:T(8,128)(2,1)S(1)}, u32[]{:S(2)}, u32[]{:S(2)}) %collective-permute-start.13) | collective-permute-done | bytes 786464 | tf_op jit(solution)/shard_map/ppermute | solution.py:169
  291.3 0.0 collective-permute-done.12.r_7_
  291.3 16.6 %collective-permute-done.9.r_4_ = bf16[512,768]{1,0:T(8,128)(2,1)} collective-permute-done((bf16[512,768]{1,0:T(8,128)(2,1)S(1)}, bf16[512,768]{1,0:T(8,128)(2,1)}, u32[]{:S(2)}, u32[]{:S(2)}) %collective-permute-start.9) | collective-permute-done | bytes 786464 | tf_op jit(solution)/shard_map/ppermute | solution.py:169
  307.9 64.5 %outproj.1 = bf16[512,6144]{1,0:T(8,128)(2,1)} custom-call(s32[2]{0:T(128)} %pad_add_fusion.r_0_, bf16[512,1536]{1,0:T(8,128)(2,1)} %copy-done.1, bf16[512,2560]{1,0:T(8,128)(2,1)} %get-tuple-element.17.r_2_, bf16[512,768]{1,0:T(8,128)(2,1)} %copy-done.6, bf16[512,768]{1,0:T(8,128)(2,1)} %collective-permute-done.9.r_4_, ...), custom_call_target="tpu_custom_call" | custom-call | flops 51999997952 | bytes 115343360 | tf_op jit(solution)/shard_map/outproj/pallas_call | solution.py:286
  (42 shorter events, 0.1 us)
Async XLA Ops:
  0.6 13.3 %slice-start = ((s8[18874368]{0:T(1024)(128)(4,1)}), s8[4194304]{0:T(1024)(128)(4,1)S(1)}, s32[]{:S(2)}) async-start(s8[18874368]{0:T(1024)(128)(4,1)} %bitcast.32), calls=%async_computation | async-start | bytes 8388608
  1.5 10.0 %copy-start.19 = (f32[32]{0:T(128)S(1)}, f32[32]{0:T(128)}, u32[]{:S(2)}) copy-start(f32[32]{0:T(128)} %constant.41.clone) | copy-start | bytes 388
  1.5 11.2 %copy-start.16 = (f32[512]{0:T(512)S(1)}, f32[512]{0:T(512)}, u32[]{:S(2)}) copy-start(f32[512]{0:T(512)} %param.18) | copy-start | bytes 6148
  1.5 12.4 %slice-start.1 = ((s8[18874368]{0:T(1024)(128)(4,1)}), s8[4194304]{0:T(1024)(128)(4,1)S(1)}, s32[]{:S(2)}) async-start(s8[18874368]{0:T(1024)(128)(4,1)} %bitcast.32), calls=%async_computation.1 | async-start | bytes 8388608
  1.5 12.4 %slice-start.2 = ((s8[18874368]{0:T(1024)(128)(4,1)}), s8[4194304]{0:T(1024)(128)(4,1)S(1)}, s32[]{:S(2)}) async-start(s8[18874368]{0:T(1024)(128)(4,1)} %bitcast.32), calls=%async_computation.2 | async-start | bytes 8388608
  1.5 12.4 %slice-start.3 = ((s8[18874368]{0:T(1024)(128)(4,1)}), s8[4194304]{0:T(1024)(128)(4,1)S(1)}, s32[]{:S(2)}) async-start(s8[18874368]{0:T(1024)(128)(4,1)} %bitcast.32), calls=%async_computation.3 | async-start | bytes 8388608
  1.5 12.4 %slice-start.4 = ((s8[18874368]{0:T(1024)(128)(4,1)}), s8[2097152]{0:T(1024)(128)(4,1)S(1)}, s32[]{:S(2)}) async-start(s8[18874368]{0:T(1024)(128)(4,1)} %bitcast.32), calls=%async_computation.4 | async-start | bytes 4194304
  12.7 0.7 copy-start.9
  12.7 0.7 copy-start.11
  12.9 0.8 copy-start.7
  27.4 3.6 copy-start.14
  30.9 55.3 %copy-start.15 = (s32[512]{0:T(512)S(1)}, s32[512]{0:T(512)}, u32[]{:S(2)}) copy-start(s32[512]{0:T(512)} %param.13) | copy-start | bytes 6148
  33.2 67.0 %copy-start.2 = (bf16[1536,512]{1,0:T(8,128)(2,1)}, bf16[1536,512]{1,0:T(8,128)(2,1)S(1)}, u32[]{:S(2)}) copy-start(bf16[1536,512]{1,0:T(8,128)(2,1)S(1)} %fusion.r_8_) | copy-start | bytes 4718596
  33.2 73.6 %collective-permute-start.7 = (bf16[1536,512]{1,0:T(8,128)(2,1)S(1)}, bf16[1536,512]{1,0:T(8,128)(2,1)}, u32[]{:S(2)}, u32[]{:S(2)}) collective-permute-start(bf16[1536,512]{1,0:T(8,128)(2,1)S(1)} %fusion.r_8_), channel_id=1, source_target_pairs={{2,0},{3,1},{6,4},{7,5}} | collective-permute-start | bytes 4718600 | tf_op jit(solution)/shard_map/ppermute | solution.py:169
  34.5 74.5 %collective-permute-start.3 = (bf16[1536,512]{1,0:T(8,128)(2,1)S(1)}, bf16[1536,512]{1,0:T(8,128)(2,1)}, u32[]{:S(2)}, u32[]{:S(2)}) collective-permute-start(bf16[1536,512]{1,0:T(8,128)(2,1)S(1)} %fusion.r_8_), channel_id=1, source_target_pairs={{0,1},{1,0},{2,3},{3,2},{4,5},{5,4},{6,7},{7,6}} | collective-permute-start | bytes 4718600 | tf_op jit(solution)/shard_map/ppermute | solution.py:169
  35.3 50.9 %collective-permute-start.1 = (bf16[512,640]{1,0:T(8,128)(2,1)S(1)}, bf16[512,640]{1,0:T(8,128)(2,1)S(1)}, u32[]{:S(2)}, u32[]{:S(2)}) collective-permute-start(bf16[512,640]{1,0:T(8,128)(2,1)S(1)} %maximum_maximum_fusion.r_4_), channel_id=1, source_target_pairs={{0,2},{1,3},{2,0},{3,1},{4,6},{5,7},{6,4},{7,5}} | collective-permute-start | bytes 1966088 | tf_op jit(solution)/shard_map/ppermute | solution.py:169
  38.9 70.1 %collective-permute-start = (bf16[512,640]{1,0:T(8,128)(2,1)S(1)}, bf16[512,640]{1,0:T(8,128)(2,1)S(1)}, u32[]{:S(2)}, u32[]{:S(2)}) collective-permute-start(bf16[512,640]{1,0:T(8,128)(2,1)S(1)} %maximum_maximum_fusion.r_4_), channel_id=1, source_target_pairs={{0,1},{1,0},{2,3},{3,2},{4,5},{5,4},{6,7},{7,6}} | collective-permute-start | bytes 1966088 | tf_op jit(solution)/shard_map/ppermute | solution.py:169
  86.2 22.7 %collective-permute-start.2 = (bf16[512,640]{1,0:T(8,128)(2,1)S(1)}, bf16[512,640]{1,0:T(8,128)(2,1)}, u32[]{:S(2)}, u32[]{:S(2)}) collective-permute-start(bf16[512,640]{1,0:T(8,128)(2,1)S(1)} %collective-permute-done.1.r_6_), channel_id=1, source_target_pairs={{0,1},{1,0},{2,3},{3,2},{4,5},{5,4},{6,7},{7,6}} | collective-permute-start | bytes 1966088 | tf_op jit(solution)/shard_map/ppermute | solution.py:169
  86.3 2.2 collective-permute-start.4
  88.5 0.6 copy-start.17
  89.0 3.0 collective-permute-start.6
  92.1 8.1 %copy-start.18 = (s32[512]{0:T(512)}, s32[512]{0:T(512)S(1)}, u32[]{:S(2)}) copy-start(s32[512]{0:T(512)S(1)} %collective-permute-done.6) | copy-start | bytes 6148
  92.1 12.3 %collective-permute-start.5 = (s32[512]{0:T(512)S(1)}, s32[512]{0:T(512)}, u32[]{:S(2)}, u32[]{:S(2)}) collective-permute-start(s32[512]{0:T(512)S(1)} %copy-done.15), channel_id=1, source_target_pairs={{0,2},{1,3},{2,0},{3,1},{4,6},{5,7},{6,4},{7,5}} | collective-permute-start | bytes 6152 | tf_op jit(solution)/shard_map/ppermute | solution.py:169
  92.1 3.4 copy-start
  100.2 2.0 copy-start.4
  102.2 2.0 copy-start.5
  106.8 44.7 %collective-permute-start.8 = (bf16[1536,512]{1,0:T(8,128)(2,1)}, bf16[1536,512]{1,0:T(8,128)(2,1)S(1)}, u32[]{:S(2)}, u32[]{:S(2)}) collective-permute-start(bf16[1536,512]{1,0:T(8,128)(2,1)} %collective-permute-done.7.r_10_), channel_id=1, source_target_pairs={{0,1},{1,0},{4,5},{5,4}} | collective-permute-start | bytes 4718600 | tf_op jit(solution)/shard_map/ppermute | solution.py:169
  150.3 1.2 copy-start.1
  151.5 1.3 copy-start.8
  152.8 37.2 %copy-start.3 = (bf16[1536,512]{1,0:T(8,128)(2,1)S(1)}, bf16[1536,512]{1,0:T(8,128)(2,1)}, u32[]{:S(2)}) copy-start(bf16[1536,512]{1,0:T(8,128)(2,1)} %copy-done.2) | copy-start | bytes 4718596
  189.9 85.0 %copy-start.6 = (bf16[512,768]{1,0:T(8,128)(2,1)}, bf16[512,768]{1,0:T(8,128)(2,1)S(1)}, u32[]{:S(2)}) copy-start(bf16[512,768]{1,0:T(8,128)(2,1)S(1)} %get-tuple-element.16.r_11_.r_3_) | copy-start | bytes 2359300
  190.0 87.9 %copy-start.10 = (bf16[512,32]{1,0:T(8,128)(2,1)S(1)}, bf16[512,32]{1,0:T(8,128)(2,1)}, u32[]{:S(2)}) copy-start(bf16[512,32]{1,0:T(8,128)(2,1)} %copy-done.9) | copy-start | bytes 98308
  190.0 87.9 %copy-start.12 = (bf16[512,32]{1,0:T(8,128)(2,1)S(1)}, bf16[512,32]{1,0:T(8,128)(2,1)}, u32[]{:S(2)}) copy-start(bf16[512,32]{1,0:T(8,128)(2,1)} %copy-done.11) | copy-start | bytes 98308
  255.3 52.6 %collective-permute-start.11 = (bf16[512,2560]{1,0:T(8,128)(2,1)}, bf16[512,2560]{1,0:T(8,128)(2,1)}, u32[]{:S(2)}, u32[]{:S(2)}) collective-permute-start(bf16[512,2560]{1,0:T(8,128)(2,1)} %get-tuple-element.19), channel_id=1, source_target_pairs={{0,1},{1,0},{2,3},{3,2},{4,5},{5,4},{6,7},{7,6}} | collective-permute-start | bytes 7864328 | tf_op jit(solution)/shard_map/ppermute | solution.py:169
  255.8 23.6 %collective-permute-start.10 = (bf16[512,1536]{1,0:T(8,128)(2,1)}, bf16[512,1536]{1,0:T(8,128)(2,1)}, u32[]{:S(2)}, u32[]{:S(2)}) collective-permute-start(bf16[512,1536]{1,0:T(8,128)(2,1)} %get-tuple-element.18), channel_id=1, source_target_pairs={{0,1},{1,0},{2,3},{3,2},{4,5},{5,4},{6,7},{7,6}} | collective-permute-start | bytes 4718600 | tf_op jit(solution)/shard_map/ppermute | solution.py:169
  255.9 35.4 %collective-permute-start.13 = (bf16[512,768]{1,0:T(8,128)(2,1)S(1)}, bf16[512,768]{1,0:T(8,128)(2,1)S(1)}, u32[]{:S(2)}, u32[]{:S(2)}) collective-permute-start(bf16[512,768]{1,0:T(8,128)(2,1)S(1)} %get-tuple-element.20), channel_id=1, source_target_pairs={{0,3},{1,2},{4,7},{5,6}} | collective-permute-start | bytes 2359304 | tf_op jit(solution)/shard_map/ppermute | solution.py:169
  273.4 17.9 %collective-permute-start.12 = (bf16[512,768]{1,0:T(8,128)(2,1)S(1)}, bf16[512,768]{1,0:T(8,128)(2,1)}, u32[]{:S(2)}, u32[]{:S(2)}) collective-permute-start(bf16[512,768]{1,0:T(8,128)(2,1)S(1)} %get-tuple-element.20), channel_id=1, source_target_pairs={{2,3},{3,2},{6,7},{7,6}} | collective-permute-start | bytes 2359304 | tf_op jit(solution)/shard_map/ppermute | solution.py:169
  275.0 32.9 %collective-permute-start.9 = (bf16[512,768]{1,0:T(8,128)(2,1)S(1)}, bf16[512,768]{1,0:T(8,128)(2,1)}, u32[]{:S(2)}, u32[]{:S(2)}) collective-permute-start(bf16[512,768]{1,0:T(8,128)(2,1)S(1)} %get-tuple-element.16.r_11_.r_3_), channel_id=1, source_target_pairs={{0,2},{1,3},{4,6},{5,7}} | collective-permute-start | bytes 2359304 | tf_op jit(solution)/shard_map/ppermute | solution.py:169
  291.3 16.6 %copy-start.13 = (bf16[512,768]{1,0:T(8,128)(2,1)}, bf16[512,768]{1,0:T(8,128)(2,1)S(1)}, u32[]{:S(2)}) copy-start(bf16[512,768]{1,0:T(8,128)(2,1)S(1)} %collective-permute-done.13.r_8_) | copy-start | bytes 2359300
